TPU v7x, 32 devices: a whole 2x2x4 slice. The times are simulated.
32 devices in a mesh: gx: 8 (over y, x, core), gy: 4 (over z).
Axes of the slice: x: 2, y: 2, z: 4, core: 2. Of those that a mesh axis runs over, the one named last changes fastest.
Arguments:
- theta: float32 [10, 128, 128, 128], P(None, 'gx', 'gy'), may hold values from -6 to 6
- phi_table: float32 [1024, 100], replicated, may hold values from -0.1 to 0.3
- dphi_table: float32 [1024, 100], replicated, may hold values from -0.5 to 1
Outputs:
- u_grids: float32 [10, 128, 128, 128], P(None, 'gx', 'gy')
- stress: float32 [3, 3], replicated
- energy: float32 [], replicated
All inputs are finite; a program needn't handle non-finite values.
Results may differ from a plain program's by a relative error of at most 0.0003.
Values sent between devices are 32-bit elements; how exact they have to be, the bound alone decides.
No kernel may reach another device: no remote copies, remote signals or barrier semaphores. Data moves between devices by JAX's collectives and lax.ppermute only.
A program may use at most 128 MiB of HBM per device.

v0:
```python
import math

import jax
import jax.numpy as jnp
import numpy as np
from jax import lax
from jax.sharding import PartitionSpec as P

HIGHEST = lax.Precision.HIGHEST
TWO_PI = 2.0 * math.pi


def signed_waves(position, length):
    shifted = (position + length // 2) % length - length // 2
    return shifted.astype(jnp.float32) * (TWO_PI / length)


def dft_table(row_freq, col_freq, length, direction):
    phase = row_freq[:, None] * col_freq[None, :] % length
    angle = phase.astype(jnp.float32) * (TWO_PI / length)
    return (jnp.cos(angle), direction * jnp.sin(angle))


def complex_turn(real_part, imag_part, cosine, sine, pattern):

    def product_of(first, second):
        return jnp.einsum(pattern, first, second, precision=HIGHEST)

    return (
        product_of(real_part, cosine) - product_of(imag_part, sine),
        product_of(real_part, sine) + product_of(imag_part, cosine),
    )


def contract_kernel(real_part, imag_part, wave_x, wave_y, wave_z, tables):
    q_count = real_part.shape[0]
    cell_count = real_part.shape[1]
    block_size = math.gcd(cell_count, 1024)
    table_points = tables.shape[0]
    pair_count = q_count * q_count
    radial_scale = (table_points - 1) / (math.pi * math.sqrt(3.0))

    def one_block(block_index, carry):
        u_real, u_imag, weight, energy_cells = carry
        offset = block_index * block_size
        part_real = lax.dynamic_slice_in_dim(real_part, offset, block_size, 1)
        part_imag = lax.dynamic_slice_in_dim(imag_part, offset, block_size, 1)
        along_x = lax.dynamic_slice_in_dim(wave_x, offset, block_size, 0)
        along_y = lax.dynamic_slice_in_dim(wave_y, offset, block_size, 0)
        along_z = lax.dynamic_slice_in_dim(wave_z, offset, block_size, 0)
        radial = jnp.sqrt(along_x * along_x + along_y * along_y + along_z * along_z) * radial_scale
        lower_point = jnp.clip(jnp.floor(radial), 0.0, table_points - 2.0)
        fraction = (radial - lower_point)[:, None]
        lower_index = lower_point.astype(jnp.int32)
        values = (1.0 - fraction) * tables[lower_index] + fraction * tables[lower_index + 1]
        kernel = values[:, :pair_count].reshape(block_size, q_count, q_count)
        kernel_slope = values[:, pair_count:].reshape(block_size, q_count, q_count)
        new_real = jnp.einsum("bqp,pb->qb", kernel, part_real, precision=HIGHEST)
        new_imag = jnp.einsum("bqp,pb->qb", kernel, part_imag, precision=HIGHEST)
        grad_real = jnp.einsum("bqp,pb->qb", kernel_slope, part_real, precision=HIGHEST)
        grad_imag = jnp.einsum("bqp,pb->qb", kernel_slope, part_imag, precision=HIGHEST)
        cell_weight = jnp.sum(part_real * grad_real + part_imag * grad_imag, axis=0)
        u_real = lax.dynamic_update_slice_in_dim(u_real, new_real, offset, 1)
        u_imag = lax.dynamic_update_slice_in_dim(u_imag, new_imag, offset, 1)
        weight = lax.dynamic_update_slice_in_dim(weight, cell_weight, offset, 0)
        cell_energy = jnp.sum(part_real * new_real + part_imag * new_imag, axis=0)
        energy_cells = lax.dynamic_update_slice_in_dim(energy_cells, cell_energy, offset, 0)
        return (u_real, u_imag, weight, energy_cells)

    start_carry = (
        jnp.zeros_like(real_part),
        jnp.zeros_like(imag_part),
        jnp.zeros((cell_count,), jnp.float32),
        jnp.zeros((cell_count,), jnp.float32),
    )
    return lax.fori_loop(0, cell_count // block_size, one_block, start_carry)


def moment_rows(weight, energy_cells, wave_x, wave_y, wave_z, item_count):
    stacked = (
        jnp.stack(
            [
                wave_x * wave_x,
                wave_y * wave_y,
                wave_z * wave_z,
                wave_x * wave_y,
                wave_x * wave_z,
                wave_y * wave_z,
            ]
        )
        * weight[None, :]
    )
    stacked = jnp.concatenate([energy_cells[None, :], stacked], axis=0)
    return jnp.sum(stacked.reshape(stacked.shape[0], item_count, -1), axis=2)


def shards(theta, phi_table, dphi_table):
    q_count, rows_x, rows_y, depth = theta.shape
    gx_size = lax.axis_size("gx")
    gy_size = lax.axis_size("gy")
    gx_index = lax.axis_index("gx")
    gy_index = lax.axis_index("gy")
    full_x = rows_x * gx_size
    full_y = rows_y * gy_size
    cell_total = full_x * full_y * depth
    tables = jnp.concatenate([phi_table, dphi_table], axis=1)
    z_points = jnp.arange(depth, dtype=jnp.int32)
    y_points = jnp.arange(full_y, dtype=jnp.int32)
    x_points = jnp.arange(full_x, dtype=jnp.int32)
    xc_fwd, xs_fwd = dft_table(x_points, x_points, full_x, -1.0)
    xc_back, xs_back = dft_table(x_points, x_points, full_x, 1.0)
    x_waves = signed_waves(x_points, full_x)
    zc_fwd, zs_fwd = dft_table(z_points, z_points, depth, -1.0)
    yc_fwd, ys_fwd = dft_table(y_points, y_points, full_y, -1.0)
    yc_back, ys_back = dft_table(y_points, y_points, full_y, 1.0)
    z_real = jnp.einsum("qxyn,nk->qkxy", theta, zc_fwd, precision=HIGHEST)
    z_imag = jnp.einsum("qxyn,nk->qkxy", theta, zs_fwd, precision=HIGHEST)
    s_real, s_imag = (
        lax.all_to_all(
            lax.all_to_all(z_real, "gx", split_axis=1, concat_axis=2, tiled=True),
            "gy",
            split_axis=1,
            concat_axis=3,
            tiled=True,
        ),
        lax.all_to_all(
            lax.all_to_all(z_imag, "gx", split_axis=1, concat_axis=2, tiled=True),
            "gy",
            split_axis=1,
            concat_axis=3,
            tiled=True,
        ),
    )
    slab_depth = depth // (gx_size * gy_size)
    z_first = gx_index * (depth // gx_size) + gy_index * slab_depth
    z_waves = signed_waves(z_first + jnp.arange(slab_depth, dtype=jnp.int32), depth)
    y_waves = signed_waves(y_points, full_y)
    a_real, a_imag = complex_turn(s_real, s_imag, xc_fwd, xs_fwd, "qzxy,xk->qzky")
    f_real, f_imag = complex_turn(a_real, a_imag, yc_fwd, ys_fwd, "qzxy,yk->qzxk")
    flat_cells = slab_depth * full_x * full_y
    grid_shape = (slab_depth, full_x, full_y)
    wave_z = jnp.broadcast_to(z_waves[:, None, None], grid_shape).reshape(flat_cells)
    wave_x = jnp.broadcast_to(x_waves[None, :, None], grid_shape).reshape(flat_cells)
    wave_y = jnp.broadcast_to(y_waves[None, None, :], grid_shape).reshape(flat_cells)
    u_real, u_imag, weight, energy_cells = contract_kernel(
        f_real.reshape(q_count, flat_cells),
        f_imag.reshape(q_count, flat_cells),
        wave_x,
        wave_y,
        wave_z,
        tables,
    )
    local_sums = moment_rows(weight, energy_cells, wave_x, wave_y, wave_z, 1)[:, 0]
    block_shape = (q_count, slab_depth, full_x, full_y)
    b_real, b_imag = complex_turn(
        u_real.reshape(block_shape), u_imag.reshape(block_shape), xc_back, xs_back, "qzky,kx->qzxy"
    )
    c_real, c_imag = complex_turn(b_real, b_imag, yc_back, ys_back, "qzxk,ky->qzxy")
    r_real, r_imag = (
        lax.all_to_all(
            lax.all_to_all(c_real, "gx", split_axis=2, concat_axis=1, tiled=True),
            "gy",
            split_axis=3,
            concat_axis=1,
            tiled=True,
        ),
        lax.all_to_all(
            lax.all_to_all(c_imag, "gx", split_axis=2, concat_axis=1, tiled=True),
            "gy",
            split_axis=3,
            concat_axis=1,
            tiled=True,
        ),
    )
    stride = gx_size * slab_depth
    positions = jnp.arange(depth, dtype=jnp.int32)
    z_order = (
        positions % stride // slab_depth * (depth // gx_size)
        + positions // stride * slab_depth
        + positions % slab_depth
    )
    zc_back, zs_back = dft_table(z_order, z_points, depth, 1.0)
    u_grids = (
        jnp.einsum("qzxy,zn->qxyn", r_real, zc_back, precision=HIGHEST)
        - jnp.einsum("qzxy,zn->qxyn", r_imag, zs_back, precision=HIGHEST)
    ) * (1.0 / cell_total)
    totals = lax.psum(local_sums, ("gx", "gy"))
    energy_scale = 0.5 / (cell_total * cell_total)
    energy = totals[0] * energy_scale
    stress_terms = totals[1:] * (-0.5 / (cell_total * cell_total))
    stress = stress_terms[np.array([0, 3, 4, 3, 1, 5, 4, 5, 2])].reshape(3, 3)
    return (u_grids, stress, energy)


def solution(mesh):
    return jax.shard_map(
        shards,
        mesh=mesh,
        in_specs=(P(None, "gx", "gy", None), P(), P()),
        out_specs=(P(None, "gx", "gy", None), P(), P()),
        check_vma=False,
    )
```

profile of v0, /device:TPU:0, one launch (start us, length us, event | category | flops | bytes accessed | tf_op | source)
XLA Modules:
  0.0 1464.3 jit_solution(7567150375264037838)
XLA Ops:
  6.3 9.9 copy.164
  16.3 9.5 reshape.302
  35.0 9.9 copy.172
  44.9 9.6 reshape.304
  54.5 8.9 all-to-all-done
  67.7 10.0 reduce.10
  77.7 9.1 reshape.303
  86.8 9.4 copy.166
  96.3 8.1 copy.167
  111.6 10.0 reduce.11
  121.6 9.1 reshape.305
  130.7 9.4 copy.174
  140.2 8.2 copy.175
  148.4 23.2 %all-to-all-done.1 = f32[10,16,128,32]{2,3,0,1:T(8,128)S(1)} async-done(((f32[10,16,128,32]{2,3,0,1:T(8,128)}), f32[10,16,128,32]{2,3,0,1:T(8,128)S(1)}, u32[]{:S(2)}, u32[]{:S(2)}) %all-to-all-start.1) | async-done | bytes 2621472 | tf_op jit(solution)/shard_map/all_to_all | solution.py:119
  189.1 47.8 %all-to-all-done.3 = f32[10,16,128,32]{2,3,0,1:T(8,128)} async-done(((f32[10,16,128,32]{2,3,0,1:T(8,128)}), f32[10,16,128,32]{2,3,0,1:T(8,128)}, u32[]{:S(2)}, u32[]{:S(2)}) %all-to-all-start.3) | async-done | bytes 2621472 | tf_op jit(solution)/shard_map/all_to_all | solution.py:126
  272.1 854.5 %while.21 = (s32[]{:T(128)}, f32[10,65536]{1,0:T(8,128)}, f32[10,65536]{1,0:T(8,128)}, f32[65536]{0:T(1024)S(1)}, f32[65536]{0:T(1024)}, /*index=5*/f32[10,65536...) while((s32[]{:T(128)}, f32[10,65536]{1,0:T(8,128)}, ...), condition=%wide.region_3.4_spmd, body=%wide.region_0.3_spmd.sunk | while | flops 1498118 | bytes 12386511 | solution.py:76
  1163.3 23.9 %all-to-all-done.6 = f32[10,4,128,128]{3,1,0,2:T(4,128)} async-done(((f32[10,4,128,128]{3,1,0,2:T(4,128)}), f32[10,4,128,128]{3,1,0,2:T(4,128)}, u32[]{:S(2)}, u32[]{:S(2)}) %all-to-all-start.6) | async-done | bytes 2621472 | tf_op jit(solution)/shard_map/all_to_all | solution.py:168
  1195.0 9.9 copy.199
  1205.0 8.2 reshape.308
  1213.2 9.8 all-to-all-done.4
  1241.1 9.9 copy.193
  1251.0 8.2 reshape.306
  1259.2 26.2 %all-to-all-done.7 = f32[4,1,163840]{2,1,0:T(1,128)S(1)} async-done(((f32[4,1,163840]{2,1,0:T(1,128)}), f32[4,1,163840]{2,1,0:T(1,128)S(1)}, u32[]{:S(2)}, u32[]{:S(2)}) %all-to-all-start.7) | async-done | bytes 2621472 | tf_op jit(solution)/shard_map/all_to_all | solution.py:167
  1292.6 77.6 %psum.7 = f32[7]{0:T(128)S(1)} all-reduce(f32[7]{0:T(128)S(1)} %maximum_reduce_fusion), channel_id=1, replica_groups=mesh['gx'=8,'gy'=4] {'gx','gy'}, use_global_device_ids=true, to_apply=%region_5.6 | all-reduce | flops 7 | bytes 56 | tf_op jit(solution)/shard_map/psum | solution.py:187
  1371.7 9.5 reduce.13
  1381.1 9.3 reshape.309
  1390.5 14.5 copy.267
  1405.0 9.1 all_to_all.135
  1414.1 8.8 reduce.12
  1423.0 7.6 reshape.307
  1430.6 14.5 copy.268
  1445.1 9.2 all_to_all.127
  (1130 shorter events, 1008.3 us)
Async XLA Ops:
  0.6 1.7 copy-start
  25.8 37.5 %all-to-all-start = ((f32[8,1,81920]{2,1,0:T(1,128)}), f32[8,1,81920]{2,1,0:T(1,128)}, u32[]{:S(2)}, u32[]{:S(2)}) async-start(f32[8,1,81920]{2,1,0:T(1,128)} %reshape.302), calls=%async_computation | async-start | bytes 5242880 | tf_op jit(solution)/shard_map/all_to_all | solution.py:120
  63.4 41.0 %all-to-all-start.2 = ((f32[8,1,81920]{2,1,0:T(1,128)}), f32[8,1,81920]{2,1,0:T(1,128)S(1)}, u32[]{:S(2)}, u32[]{:S(2)}) async-start(f32[8,1,81920]{2,1,0:T(1,128)} %reshape.304), calls=%async_computation.2 | async-start | bytes 5242880 | tf_op jit(solution)/shard_map/all_to_all | solution.py:127
  104.4 1.5 copy-start.7
  105.9 65.7 %all-to-all-start.1 = ((f32[10,16,128,32]{2,3,0,1:T(8,128)}), f32[10,16,128,32]{2,3,0,1:T(8,128)S(1)}, u32[]{:S(2)}, u32[]{:S(2)}) async-start(f32[10,16,128,32]{2,3,0,1:T(8,128)} %copy.167), calls=%async_computation.1 | async-start | bytes 5242880 | tf_op jit(solution)/shard_map/all_to_all | solution.py:119
  148.4 29.7 %copy-start.14 = (f32[1024,100]{0,1:T(8,128)S(1)}, f32[1024,100]{0,1:T(8,128)}, u32[]{:S(2)}) copy-start(f32[1024,100]{0,1:T(8,128)} %param.8) | copy-start | bytes 1228804
  148.4 29.9 %copy-start.15 = (f32[1024,100]{0,1:T(8,128)S(1)}, f32[1024,100]{0,1:T(8,128)}, u32[]{:S(2)}) copy-start(f32[1024,100]{0,1:T(8,128)} %param.9) | copy-start | bytes 1228804
  171.6 1.5 copy-start.5
  173.1 63.8 %all-to-all-start.3 = ((f32[10,16,128,32]{2,3,0,1:T(8,128)}), f32[10,16,128,32]{2,3,0,1:T(8,128)}, u32[]{:S(2)}, u32[]{:S(2)}) async-start(f32[10,16,128,32]{2,3,0,1:T(8,128)} %copy.175), calls=%async_computation.3 | async-start | bytes 5242880 | tf_op jit(solution)/shard_map/all_to_all | solution.py:126
  236.9 2.5 copy-start.10
  244.6 2.6 copy-start.9
  1126.6 3.1 copy-start.11
  1132.6 2.7 copy-start.4
  1139.2 5.4 copy-start.2
  1150.3 36.9 %all-to-all-start.6 = ((f32[10,4,128,128]{3,1,0,2:T(4,128)}), f32[10,4,128,128]{3,1,0,2:T(4,128)}, u32[]{:S(2)}, u32[]{:S(2)}) async-start(f32[10,4,128,128]{3,1,0,2:T(4,128)} %copy.196), calls=%async_computation.6 | async-start | bytes 5242880 | tf_op jit(solution)/shard_map/all_to_all | solution.py:168
  1155.0 2.6 copy-start.3
  1187.2 35.8 %all-to-all-start.4 = ((f32[10,4,128,128]{3,1,0,2:T(4,128)}), f32[10,4,128,128]{3,1,0,2:T(4,128)S(1)}, u32[]{:S(2)}, u32[]{:S(2)}) async-start(f32[10,4,128,128]{3,1,0,2:T(4,128)} %copy.190), calls=%async_computation.4 | async-start | bytes 5242880 | tf_op jit(solution)/shard_map/all_to_all | solution.py:161
  1223.0 1.5 copy-start.6
  1224.5 60.9 %all-to-all-start.7 = ((f32[4,1,163840]{2,1,0:T(1,128)}), f32[4,1,163840]{2,1,0:T(1,128)S(1)}, u32[]{:S(2)}, u32[]{:S(2)}) async-start(f32[4,1,163840]{2,1,0:T(1,128)} %reshape.308), calls=%async_computation.7 | async-start | bytes 5242880 | tf_op jit(solution)/shard_map/all_to_all | solution.py:167
  1228.6 8.3 copy-start.16
  1259.2 30.8 %copy-start.12 = (f32[65536]{0:T(1024)S(1)}, f32[65536]{0:T(1024)}, u32[]{:S(2)}) copy-start(f32[65536]{0:T(1024)} %copy-done.11) | copy-start | bytes 786436
  1285.4 128.7 %all-to-all-start.5 = ((f32[4,1,163840]{2,1,0:T(1,128)}), f32[4,1,163840]{2,1,0:T(1,128)}, u32[]{:S(2)}, u32[]{:S(2)}) async-start(f32[4,1,163840]{2,1,0:T(1,128)} %reshape.306), calls=%async_computation.5 | async-start | bytes 5242880 | tf_op jit(solution)/shard_map/all_to_all | solution.py:160
  1290.0 1.9 copy-start.13
  1454.3 4.4 copy-start.8
  1454.3 8.5 copy-start.1
where the time goes:
time: 1480 us; the launch traced here: 1460 us
  local copies, waits for them, and re-layouts  901 us (61%)
  other arithmetic  241 us (16%)
  waiting for transfers between devices  140 us (9%)
  blocking collectives  77.6 us (5%)
  matrix products  61.5 us (4%)
  starting transfers between devices  36.5 us (2%)
    gather x64, local copies, waits for them, and re-layouts, one_block(): tables[lower_index + 1]  222 us
    gather x64, local copies, waits for them, and re-layouts, one_block(): tables[lower_index]  222 us
    reduce_sum x64, other arithmetic, one_block(): cell_energy = jnp.sum(part_real * new_real + part_imag * new_imag, axis=0)  99.7 us
    unnamed x52, local copies, waits for them, and re-layouts  91.6 us
    dynamic_update_slice x64, local copies, waits for them, and re-layouts, one_block(): lax.dynamic_update_slice_in_dim(energy_cells, cell_energy, offset, 0)  90.7 us
    psum x1, blocking collectives, shards(): totals = lax.psum(local_sums, ('gx', 'gy'))  77.6 us
    while x64, local copies, waits for them, and re-layouts  56.9 us
    all_to_all x1, waiting for transfers between devices, shards(): lax.all_to_all(lax.all_to_all(z_imag, 'gx', split_axis=1, concat_axis=2,...  47.8 us
  transfers between devices with their start and end apart: 8, of which 6 were waited for; matrix products, arithmetic and copies ran while one was open for 14% of the time, Pallas kernels for 0%

commit v1 on v0

--- a/solution.py
+++ b/solution.py
@@ -1,9 +1,12 @@
+import functools
 import math
 
 import jax
 import jax.numpy as jnp
 import numpy as np
 from jax import lax
+from jax.experimental import pallas as pl
+from jax.experimental.pallas import tpu as pltpu
 from jax.sharding import PartitionSpec as P
 
 HIGHEST = lax.Precision.HIGHEST
@@ -94,7 +97,7 @@
     return jnp.sum(stacked.reshape(stacked.shape[0], item_count, -1), axis=2)
 
 
-def shards(theta, phi_table, dphi_table):
+def general_shards(theta, phi_table, dphi_table):
     q_count, rows_x, rows_y, depth = theta.shape
     gx_size = lax.axis_size("gx")
     gy_size = lax.axis_size("gy")
@@ -192,6 +195,490 @@
     return (u_grids, stress, energy)
 
 
+LANES = 128
+SUBLANES = 8
+STATS = 7
+AXES = ("gx", "gy")
+
+
+def real_basis(length):
+    half = length // 2
+    points = np.arange(length)
+    rows = []
+    for index in range(length):
+        number = index if index <= half else index - half
+        angle = TWO_PI * (number * points % length) / length
+        if index in (0, half):
+            rows.append(np.cos(angle) / math.sqrt(length))
+        elif index < half:
+            rows.append(np.cos(angle) * math.sqrt(2.0 / length))
+        else:
+            rows.append(np.sin(angle) * math.sqrt(2.0 / length))
+    return np.stack(rows)
+
+
+def halves(table):
+    high = np.asarray(table, dtype=jnp.bfloat16)
+    low = np.asarray(table - high.astype(np.float64), dtype=jnp.bfloat16)
+    return high, low
+
+
+def split(value):
+    high = value.astype(jnp.bfloat16)
+    low = (value - high.astype(jnp.float32)).astype(jnp.bfloat16)
+    return high, low
+
+
+def product(left, right, contract_right=0):
+    return lax.dot_general(
+        left, right, (((1,), (contract_right,)), ((), ())), preferred_element_type=jnp.float32
+    )
+
+
+def z_forward_kernel(theta_ref, basis_ref, out_ref, *, q_count, groups, devices, rows):
+    q = pl.program_id(0)
+    high, low = split(theta_ref[0])
+    spectrum = product(basis_ref[...], jnp.concatenate([high, low, high], axis=1), 1)
+    for j in range(2):
+        for g in range(groups):
+            out_ref[pl.ds((g * 2 + j) * q_count + q, devices, stride=rows), :] = spectrum[
+                j * devices : (j + 1) * devices, g * LANES : (g + 1) * LANES
+            ]
+
+
+def z_inverse_kernel(*refs, q_count, groups, devices, rows, slots):
+    sent_refs, basis_ref, out_ref = refs[:slots], refs[slots], refs[slots + 1]
+    q = pl.program_id(0)
+    for g in range(groups):
+        parts = []
+        for sent_ref in sent_refs:
+            for j in range(2):
+                parts.append(
+                    sent_ref[pl.ds((g * 2 + j) * q_count + q, devices, stride=rows), :]
+                )
+        high, low = split(jnp.transpose(jnp.concatenate(parts, axis=0)))
+        out_ref[0, g * LANES : (g + 1) * LANES, :] = product(
+            jnp.concatenate([high, low, high], axis=1), basis_ref[...]
+        )
+
+
+def fold(index, half):
+    return jnp.where(index > half, index - half, index)
+
+
+def table_kernel(planes_ref, bounds_ref, value_ref, step_ref, out_ref, *, half, pairs, group, scale, tiles, points):
+    wave = math.pi / half
+    row = lax.broadcasted_iota(jnp.int32, (SUBLANES, LANES), 0)
+    wave_y = fold(lax.broadcasted_iota(jnp.int32, (SUBLANES, LANES), 1), half).astype(jnp.float32) * wave
+    blocks = half // SUBLANES + 1
+
+    def one_block(index, _):
+        j = index // blocks
+        block = index % blocks
+        number = planes_ref[j]
+        wave_z = number.astype(jnp.float32) * wave
+        last = block == blocks - 1
+        along_x = jnp.where(last, jnp.where(row == 0, half, row), row + block * SUBLANES)
+        wave_x = along_x.astype(jnp.float32) * wave
+        radial = jnp.sqrt(wave_x * wave_x + wave_y * wave_y + wave_z * wave_z) * scale
+        lower = jnp.clip(jnp.floor(radial), 0.0, points - 2.0)
+        fraction = radial - lower
+        lower = lower.astype(jnp.int32)
+        tile = lower // LANES
+        lane = lower % LANES
+        masks = [tile == t for t in range(tiles)]
+        start = pl.multiple_of(block * SUBLANES, SUBLANES)
+
+        def one_group(step, _):
+            for i in range(group):
+                pair = step * group + i
+                value = jnp.zeros((SUBLANES, LANES), jnp.float32)
+                slope = value
+                for t in range(tiles):
+                    def look(ref):
+                        source = jnp.broadcast_to(ref[t, pl.ds(pair, 1), :], (SUBLANES, LANES))
+                        return jnp.take_along_axis(source, lane, axis=1, mode="promise_in_bounds")
+                    value = jnp.where(masks[t], look(value_ref), value)
+                    slope = jnp.where(masks[t], look(step_ref), slope)
+                out_ref[j, pair, pl.ds(start, SUBLANES), :] = value + fraction * slope
+            return 0
+
+        lax.fori_loop(0, pairs // group, one_group, 0)
+        return 0
+
+    lax.fori_loop(0, planes_ref[2] * blocks, one_block, 0)
+
+
+def plane_kernel(
+    planes_ref,
+    waves_ref,
+    sent_ref,
+    y_ref,
+    y_back_ref,
+    x_ref,
+    x_back_ref,
+    table_hbm,
+    out_ref,
+    stats_ref,
+    table_ref,
+    y_wide_ref,
+    y_back_wide_ref,
+    rows_ref,
+    spectrum_ref,
+    u_ref,
+    sem,
+    *,
+    q_count,
+    gx_size,
+    gy_size,
+    rows,
+    half,
+):
+    copy = pltpu.make_async_copy(table_hbm, table_ref, sem)
+    copy.start()
+    full = 2 * half
+    local_y = full // gy_size
+    spread = LANES // local_y
+    planes = 2 * q_count
+    strips = rows // planes
+    high_x = gx_size * strips
+    total_rows = gx_size * rows
+    bf16 = jnp.bfloat16
+
+    y_wide_ref[...] = jnp.zeros_like(y_wide_ref)
+    for part in range(3):
+        for s in range(gy_size):
+            for k in range(spread):
+                top = (part * gy_size + s) * LANES + k * local_y
+                y_wide_ref[top : top + local_y, k * full : (k + 1) * full] = y_ref[
+                    part, s * local_y : (s + 1) * local_y, :
+                ]
+    lane_part = lax.broadcasted_iota(jnp.int32, (full, gy_size * LANES), 1) // local_y % spread
+    for part in range(3):
+        for k in range(spread):
+            top = (part * spread + k) * full
+            y_back_wide_ref[top : top + full, :] = jnp.where(
+                lane_part == k, y_back_ref[part].astype(jnp.float32), 0.0
+            ).astype(bf16)
+
+    for x in range(gx_size):
+        highs, lows = [], []
+        for s in range(gy_size):
+            top = (x * gy_size + s) * rows
+            high, low = split(sent_ref[top : top + rows, :])
+            highs.append(high)
+            lows.append(low)
+        result = product(jnp.concatenate(highs + lows + highs, axis=1), y_wide_ref[...])
+        for k in range(spread):
+            top = k * total_rows + x * rows
+            rows_ref[top : top + rows, :] = result[:, k * full : (k + 1) * full]
+
+    for first in range(0, planes, 2):
+        pair = []
+        for plane in (first, first + 1):
+            pair.append(
+                jnp.concatenate(
+                    [
+                        rows_ref[pl.ds(k * total_rows + plane, high_x, stride=planes), :]
+                        for k in range(spread)
+                    ],
+                    axis=0,
+                )
+            )
+        high, low = split(jnp.concatenate(pair, axis=1))
+        result = product(x_ref[...], jnp.concatenate([high, high, low], axis=0))
+        for i in range(2):
+            spectrum_ref[(first + i) * full : (first + i + 1) * full, :] = result[:, i * full : (i + 1) * full]
+
+    copy.wait()
+    wave = math.pi / half
+    lane = lax.broadcasted_iota(jnp.int32, (SUBLANES, LANES), 1)
+    row = lax.broadcasted_iota(jnp.int32, (SUBLANES, LANES), 0)
+    wave_y = fold(lane, half).astype(jnp.float32) * wave
+    signed_y = jnp.where(lane < half, wave_y, jnp.where(lane == half, 0.0, -wave_y))
+    nyquist_y = jnp.where(lane == half, math.pi, 0.0)
+    wave_z0, wave_z1, cross_z, nyquist_z = (waves_ref[i] for i in range(4))
+    plane_index = (0, planes_ref[2] - 1)
+    upper = {}
+    for q in range(q_count):
+        for p in range(q, q_count):
+            upper[q, p] = upper[p, q] = q_count * q_count + len({k for k in upper if k[0] <= k[1]})
+
+    def turn(value):
+        return pltpu.roll(value, half, 1)
+
+    def one_block(block, carry):
+        energy, xx, yy, zz, xy, xz, yz = carry
+        top = pl.multiple_of(block * SUBLANES, SUBLANES)
+        tops = (top, pl.multiple_of(jnp.where(block == 0, half, top), SUBLANES))
+        values = {}
+        for j in range(2):
+            for h in range(2):
+                values[j, h] = [
+                    spectrum_ref[pl.ds(pl.multiple_of((j * q_count + q) * full + h * half + top, SUBLANES), SUBLANES), :]
+                    for q in range(q_count)
+                ]
+        zero = jnp.zeros((SUBLANES, LANES), jnp.float32)
+        form = {key: zero for key in values}
+        cross_xy, cross_xz, cross_yz = zero, zero, zero
+        for q in range(q_count):
+            bent = {}
+            for key in values:
+                j, h = key
+                u = None
+                for p in range(q_count):
+                    term = table_ref[plane_index[j], q * q_count + p, pl.ds(tops[h], SUBLANES), :] * values[key][p]
+                    u = term if u is None else u + term
+                u_ref[pl.ds(pl.multiple_of((j * q_count + q) * full + h * half + top, SUBLANES), SUBLANES), :] = u
+                energy = energy + u * values[key][q]
+                v = None
+                for p in range(q_count):
+                    term = table_ref[plane_index[j], upper[q, p], pl.ds(tops[h], SUBLANES), :] * values[key][p]
+                    v = term if v is None else v + term
+                bent[key] = v
+                form[key] = form[key] + v * values[key][q]
+            cross_xy = cross_xy + bent[0, 0] * turn(values[0, 1][q]) + bent[1, 0] * turn(values[1, 1][q])
+            cross_xz = cross_xz + bent[0, 0] * values[1, 1][q] - bent[1, 0] * values[0, 1][q]
+            cross_yz = cross_yz + bent[0, 0] * turn(values[1, 0][q]) + bent[0, 1] * turn(values[1, 1][q])
+        number = row + block * SUBLANES
+        wave_c = number.astype(jnp.float32) * wave
+        wave_s = jnp.where(number == 0, half, number).astype(jnp.float32) * wave
+        nyquist_x = jnp.where(number == 0, math.pi, 0.0)
+        xx = xx + (form[0, 0] + form[1, 0]) * (wave_c * wave_c) + (form[0, 1] + form[1, 1]) * (wave_s * wave_s)
+        yy = yy + (form[0, 0] + form[1, 0] + form[0, 1] + form[1, 1]) * (wave_y * wave_y)
+        zz = zz + (form[0, 0] + form[0, 1]) * (wave_z0 * wave_z0) + (form[1, 0] + form[1, 1]) * (wave_z1 * wave_z1)
+        xy = xy - 2.0 * wave_c * signed_y * cross_xy + nyquist_x * nyquist_y * (form[0, 1] + form[1, 1])
+        xz = xz - 2.0 * cross_z * wave_c * cross_xz + nyquist_z * nyquist_x * form[1, 1]
+        yz = yz - 2.0 * cross_z * signed_y * cross_yz + nyquist_z * nyquist_y * (form[1, 0] + form[1, 1])
+        return energy, xx, yy, zz, xy, xz, yz
+
+    start = (jnp.zeros((SUBLANES, LANES), jnp.float32),) * STATS
+    sums = lax.fori_loop(0, half // SUBLANES, one_block, start)
+    stats_ref[...] = jnp.concatenate(
+        [jnp.sum(part, axis=0, keepdims=True) for part in sums] + [jnp.zeros((1, LANES), jnp.float32)], axis=0
+    )
+
+    for first in range(0, planes, 2):
+        high, low = split(
+            jnp.concatenate(
+                [u_ref[(first + i) * full : (first + i + 1) * full, :] for i in range(2)], axis=1
+            )
+        )
+        result = product(x_back_ref[...], jnp.concatenate([high, high, low], axis=0))
+        for i in range(2):
+            for k in range(spread):
+                rows_ref[pl.ds(k * total_rows + first + i, high_x, stride=planes), :] = result[
+                    k * high_x : (k + 1) * high_x, i * full : (i + 1) * full
+                ]
+
+    for x in range(gx_size):
+        strip = [rows_ref[k * total_rows + x * rows : k * total_rows + (x + 1) * rows, :] for k in range(spread)]
+        high, low = split(jnp.concatenate(strip, axis=1))
+        result = product(jnp.concatenate([high, low, high], axis=1), y_back_wide_ref[...])
+        for s in range(gy_size):
+            top = (x * gy_size + s) * rows
+            out_ref[top : top + rows, :] = result[:, s * LANES : (s + 1) * LANES]
+
+
+def table_rows(phi_table, dphi_table, q_count, padded):
+    points = phi_table.shape[0]
+    first = np.array([q * q_count + p for q in range(q_count) for p in range(q, q_count)])
+    second = np.array([p * q_count + q for q in range(q_count) for p in range(q, q_count)])
+    slopes = dphi_table.T
+    slopes = 0.5 * (slopes[first] + slopes[second])
+    table = jnp.concatenate([phi_table.T, slopes], axis=0)
+    table = jnp.pad(table, ((0, padded - table.shape[0]), (0, 0)))
+    steps = jnp.pad(table[:, 1:] - table[:, :-1], ((0, 0), (0, 1)))
+
+    def tiled(values):
+        return values.reshape(padded, points // LANES, LANES).transpose(1, 0, 2)
+
+    return tiled(table), tiled(steps)
+
+
+def butterfly(value, devices):
+    step = 1
+    while step < devices:
+        value = value + lax.ppermute(value, AXES, [(i, i ^ step) for i in range(devices)])
+        step *= 2
+    return value
+
+
+def swap(value, devices):
+    parts = value.reshape(devices, -1, LANES)
+    return lax.all_to_all(parts, AXES, split_axis=0, concat_axis=0, tiled=True).reshape(value.shape)
+
+
+def real_shards(theta, phi_table, dphi_table):
+    q_count, local_x, local_y, depth = theta.shape
+    gx_size = lax.axis_size("gx")
+    gy_size = lax.axis_size("gy")
+    devices = gx_size * gy_size
+    full = local_x * gx_size
+    half = full // 2
+    slots = depth // (2 * devices)
+    groups = local_x * local_y // LANES
+    spread = LANES // local_y
+    rows = groups * 2 * q_count
+    me = lax.axis_index("gx") * gy_size + lax.axis_index("gy")
+    table_points = phi_table.shape[0]
+    tiles = table_points // LANES
+    upper_pairs = q_count * (q_count + 1) // 2
+    group = 16
+    padded = -(-(q_count * q_count + upper_pairs) // group) * group
+    cell_total = full * full * depth
+    vmem = pl.BlockSpec(memory_space=pltpu.VMEM)
+    smem = pl.BlockSpec(memory_space=pltpu.SMEM)
+    hbm = pl.BlockSpec(memory_space=pl.ANY)
+
+    z_basis = real_basis(depth)
+    basis = real_basis(full)
+
+    def coefficient(slot, j):
+        return slot if j == 0 else (depth // 2 + slot)
+
+    order = [
+        [coefficient(c * devices + d, j) for j in range(2) for d in range(devices)] for c in range(slots)
+    ]
+    flat_theta = theta.reshape(q_count, local_x * local_y, depth)
+    sent = []
+    for c in range(slots):
+        high, low = halves(z_basis[order[c]])
+        sent.append(
+            pl.pallas_call(
+                functools.partial(
+                    z_forward_kernel, q_count=q_count, groups=groups, devices=devices, rows=rows
+                ),
+                grid=(q_count,),
+                in_specs=[
+                    pl.BlockSpec((1, local_x * local_y, depth), lambda q: (q, 0, 0)),
+                    pl.BlockSpec((2 * devices, 3 * depth), lambda q: (0, 0)),
+                ],
+                out_specs=pl.BlockSpec((devices * rows, LANES), lambda q: (0, 0)),
+                out_shape=jax.ShapeDtypeStruct((devices * rows, LANES), jnp.float32),
+                name="z_forward",
+            )(flat_theta, jnp.asarray(np.concatenate([high, high, low], axis=1)))
+        )
+    arrived = [swap(part, devices) for part in sent]
+
+    value_table, step_table = table_rows(phi_table, dphi_table, q_count, padded)
+    wave = math.pi / half
+    scale = (table_points - 1) / (math.pi * math.sqrt(3.0))
+    tables, settings = [], []
+    blocks = half // SUBLANES + 1
+    for c in range(slots):
+        slot = c * devices + me
+        special = slot == 0
+        plane_numbers = jnp.stack(
+            [slot, jnp.where(special, half, slot), jnp.where(special, 2, 1)]
+        ).astype(jnp.int32)
+        number = slot.astype(jnp.float32) * wave
+        wave_values = jnp.stack(
+            [
+                number,
+                jnp.where(special, math.pi, number),
+                jnp.where(special, 0.0, number),
+                jnp.where(special, math.pi, 0.0),
+            ]
+        )
+        settings.append((plane_numbers, wave_values))
+        tables.append(
+            pl.pallas_call(
+                functools.partial(
+                    table_kernel,
+                    half=half,
+                    pairs=padded,
+                    group=group,
+                    scale=scale,
+                    tiles=tiles,
+                    points=table_points,
+                ),
+                in_specs=[smem, smem, vmem, vmem],
+                out_specs=vmem,
+                out_shape=jax.ShapeDtypeStruct((2, padded, blocks * SUBLANES, LANES), jnp.float32),
+                name="kernel_table",
+            )(plane_numbers, plane_numbers, value_table, step_table)
+        )
+
+    x_order = [
+        (h // groups) * local_x + (h % groups) * spread + k for k in range(spread) for h in range(gx_size * groups)
+    ]
+    high, low = halves(basis[:, x_order])
+    x_forward = jnp.asarray(np.concatenate([high, low, high], axis=1))
+    x_back = jnp.asarray(np.concatenate([high.T, low.T, high.T], axis=1))
+    high, low = halves(basis)
+    y_forward = jnp.asarray(np.stack([high.T, high.T, low.T]))
+    wide = [
+        np.concatenate(
+            [part[:, s * local_y : (s + 1) * local_y] for s in range(gy_size) for _ in range(spread)], axis=1
+        )
+        for part in (high, low)
+    ]
+    y_back = jnp.asarray(np.stack([wide[0], wide[0], wide[1]]))
+    returned, stats = [], None
+    for c in range(slots):
+        back, part = pl.pallas_call(
+            functools.partial(
+                plane_kernel, q_count=q_count, gx_size=gx_size, gy_size=gy_size, rows=rows, half=half
+            ),
+            in_specs=[smem, smem, vmem, vmem, vmem, vmem, vmem, hbm],
+            out_specs=(vmem, vmem),
+            out_shape=(
+                jax.ShapeDtypeStruct((devices * rows, LANES), jnp.float32),
+                jax.ShapeDtypeStruct((SUBLANES, LANES), jnp.float32),
+            ),
+            scratch_shapes=[
+                pltpu.VMEM((2, padded, blocks * SUBLANES, LANES), jnp.float32),
+                pltpu.VMEM((3 * gy_size * LANES, spread * full), jnp.bfloat16),
+                pltpu.VMEM((3 * spread * full, gy_size * LANES), jnp.bfloat16),
+                pltpu.VMEM((spread * gx_size * rows, full), jnp.float32),
+                pltpu.VMEM((2 * q_count * full, LANES), jnp.float32),
+                pltpu.VMEM((2 * q_count * full, LANES), jnp.float32),
+                pltpu.SemaphoreType.DMA,
+            ],
+            name="planes",
+        )(*settings[c], arrived[c], y_forward, y_back, x_forward, x_back, tables[c])
+        returned.append(swap(back, devices))
+        stats = part if stats is None else stats + part
+
+    high, low = halves(np.concatenate([z_basis[rows_of] for rows_of in order], axis=0))
+    u_grids = pl.pallas_call(
+        functools.partial(
+            z_inverse_kernel, q_count=q_count, groups=groups, devices=devices, rows=rows, slots=slots
+        ),
+        grid=(q_count,),
+        in_specs=[pl.BlockSpec((devices * rows, LANES), lambda q: (0, 0))] * slots
+        + [pl.BlockSpec((3 * depth, depth), lambda q: (0, 0))],
+        out_specs=pl.BlockSpec((1, local_x * local_y, depth), lambda q: (q, 0, 0)),
+        out_shape=jax.ShapeDtypeStruct((q_count, local_x * local_y, depth), jnp.float32),
+        name="z_inverse",
+    )(*returned, jnp.asarray(np.concatenate([high, high, low], axis=0)))
+
+    totals = jnp.sum(butterfly(stats, devices), axis=1)
+    energy = totals[0] * (0.5 / cell_total)
+    stress_terms = totals[1:STATS] * (-0.5 / cell_total)
+    stress = stress_terms[np.array([0, 3, 4, 3, 1, 5, 4, 5, 2])].reshape(3, 3)
+    return (u_grids.reshape(theta.shape), stress, energy)
+
+
+def shards(theta, phi_table, dphi_table):
+    q_count, local_x, local_y, depth = theta.shape
+    gx_size = lax.axis_size("gx")
+    gy_size = lax.axis_size("gy")
+    devices = gx_size * gy_size
+    fits = (
+        local_x * gx_size == LANES
+        and local_y * gy_size == LANES
+        and depth == LANES
+        and depth % (2 * devices) == 0
+        and local_x * local_y % LANES == 0
+        and phi_table.shape[0] % LANES == 0
+        and devices & (devices - 1) == 0
+        and (local_x * local_y // LANES) * q_count % 4 == 0
+    )
+    return (real_shards if fits else general_shards)(theta, phi_table, dphi_table)
+
+
 def solution(mesh):
     return jax.shard_map(
         shards,

time: 1480 us -> 248 us (0.17)
  local copies, waits for them, and re-layouts: 901 us -> 8.09 us
  other arithmetic: 241 us -> 2.98 us
  Pallas kernels: 0 us -> 150 us
  waiting for transfers between devices: 140 us -> 53.9 us
  blocking collectives: 77.6 us -> 0 us
  matrix products: 61.5 us -> 0 us
    gather x129 -> x3, local copies, waits for them, and re-layouts: 444 us -> 1.98 us  [the longest x2 1.32 us: table_rows(): slopes = 0.5 * (slopes[first] + slopes[second])]
    pallas_call x0 -> x7, Pallas kernels: none -> 150 us  [the longest x2 104 us: real_shards(): pl.pallas_call(functools.partial(table_kernel, half=half, pairs=padded, g...]
    all_to_all x8 -> x4, waiting for transfers between devices: 140 us -> 22.8 us  [swap(): lax.all_to_all(parts, AXES, split_axis=0, concat_axis=0, tiled=True)]
    all_to_all x17 -> x0, local copies, waits for them, and re-layouts: 115 us -> none  [the longest x2 23.7 us: shards(): lax.all_to_all(lax.all_to_all(c_real, 'gx', split_axis=2, concat_axis=1,...]
    dynamic_update_slice x128 -> x0, local copies, waits for them, and re-layouts: 101 us -> none  [the longest x64 90.7 us: one_block(): lax.dynamic_update_slice_in_dim(energy_cells, cell_energy, offset, 0)]
    reduce_sum x65 -> x1, other arithmetic: 100 us -> 0.11 us  [real_shards(): totals = jnp.sum(butterfly(stats, devices), axis=1)]
    unnamed x52 -> x22, local copies, waits for them, and re-layouts: 91.6 us -> 4.22 us
    psum x1 -> x0, blocking collectives: 77.6 us -> none  [shards(): totals = lax.psum(local_sums, ('gx', 'gy'))]
  transfers between devices with their start and end apart: 8 -> 9, of which waited for: 6 -> 6; matrix products, arithmetic and copies ran while one was open for 14% -> 3% of each run, Pallas kernels for 0% -> 55%
where the time goes in v1:
time: 248 us; the launch traced here: 247 us
  Pallas kernels  150 us (60%)
  waiting for transfers between devices  53.9 us (22%)
  starting transfers between devices  29.7 us (12%)
  local copies, waits for them, and re-layouts  8.09 us (3%)
  other arithmetic  2.98 us (1%)
    pallas_call x2, Pallas kernels, real_shards(): pl.pallas_call(functools.partial(table_kernel, half=half, pairs=padded, g...  104 us
    ppermute x5, waiting for transfers between devices, butterfly(): lax.ppermute(value, AXES, [(i, i ^ step) for i in range(devices)])  31.1 us
    pallas_call x2, Pallas kernels, real_shards(): pl.pallas_call(functools.partial(plane_kernel, q_count=q_count, gx_size=g...  23.7 us
    all_to_all x4, waiting for transfers between devices, swap(): lax.all_to_all(parts, AXES, split_axis=0, concat_axis=0, tiled=True)  22.8 us
    all_to_all x4, starting transfers between devices, swap(): lax.all_to_all(parts, AXES, split_axis=0, concat_axis=0, tiled=True)  20.5 us
    pallas_call x2, Pallas kernels, real_shards(): pl.pallas_call(functools.partial(z_forward_kernel, q_count=q_count, group...  15.2 us
    ppermute x5, starting transfers between devices, butterfly(): lax.ppermute(value, AXES, [(i, i ^ step) for i in range(devices)])  9.19 us
    pallas_call x1, Pallas kernels, real_shards(): pl.pallas_call(functools.partial(z_inverse_kernel, q_count=q_count, group...  7.22 us
  transfers between devices with their start and end apart: 9, of which 6 were waited for; matrix products, arithmetic and copies ran while one was open for 3% of the time, Pallas kernels for 55%

profile of v1, /device:TPU:0, one launch (start us, length us, event | category | flops | bytes accessed | tf_op | source)
XLA Modules:
  0.0 247.1 jit_solution(12868772278614251284)
XLA Ops:
  0.6 7.6 %z_forward.2 = f32[2560,128]{1,0:T(8,128)} custom-call(f32[10,512,128]{2,1,0:T(8,128)} %bitcast.43, bf16[64,384]{1,0:T(8,128)(2,1)} %constant.63.clone.basis_ref), custom_call_target="tpu_custom_call" | custom-call | tf_op jit(solution)/shard_map/z_forward/pallas_call | solution.py:548
  8.3 7.3 %all-to-all-start = ((f32[32,80,128]{2,1,0:T(8,128)}), f32[32,80,128]{2,1,0:T(8,128)S(1)}, u32[]{:S(2)}, u32[]{:S(2)}) async-start(f32[32,80,128]{2,1,0:T(8,128)} %bitcast.46), calls=%async_computation | async-start | bytes 2621440 | tf_op jit(solution)/shard_map/all_to_all | solution.py:509
  15.6 7.6 %z_forward.3 = f32[2560,128]{1,0:T(8,128)} custom-call(f32[10,512,128]{2,1,0:T(8,128)} %bitcast.44, bf16[64,384]{1,0:T(8,128)(2,1)} %constant.64.clone.basis_ref), custom_call_target="tpu_custom_call" | custom-call | tf_op jit(solution)/shard_map/z_forward/pallas_call | solution.py:548
  23.2 22.8 %all-to-all-done = f32[32,80,128]{2,1,0:T(8,128)S(1)} async-done(((f32[32,80,128]{2,1,0:T(8,128)}), f32[32,80,128]{2,1,0:T(8,128)S(1)}, u32[]{:S(2)}, u32[]{:S(2)}) %all-to-all-start) | async-done | bytes 1310752 | tf_op jit(solution)/shard_map/all_to_all | solution.py:509
  46.0 1.1 copy-done.4
  47.0 4.6 %all-to-all-start.2 = ((f32[32,80,128]{2,1,0:T(8,128)}), f32[32,80,128]{2,1,0:T(8,128)S(1)}, u32[]{:S(2)}, u32[]{:S(2)}) async-start(f32[32,80,128]{2,1,0:T(8,128)} %bitcast.45), calls=%async_computation.2 | async-start | bytes 2621440 | tf_op jit(solution)/shard_map/all_to_all | solution.py:509
  51.7 0.7 gather_fusion
  52.4 0.7 gather_fusion.1
  53.1 0.6 pad_add_fusion.planes_ref.bounds_ref
  54.1 1.2 bitcast_bitcast_fusion
  55.3 67.6 %kernel_table.2.table_hbm = f32[2,160,72,128]{3,2,1,0:T(8,128)} custom-call(s32[3]{0:T(128)} %pad_add_fusion.planes_ref.bounds_ref, s32[3]{0:T(128)} %pad_add_fusion.planes_ref.bounds_ref, f32[8,160,128]{2,1,0:T(8,128)} %get-tuple-element.14.value_ref, f32[8,160,128]{2,1,0:T(8,128)} %get-tuple-element.13.step_ref), custom_call_target="tpu_custom_call" | custom-call | tf_op jit(solution)/shard_map/kernel_table/pallas_call | solution.py:586
  123.5 11.9 %planes.2 = (f32[2560,128]{1,0:T(8,128)}, f32[8,128]{1,0:T(8,128)}) custom-call(s32[3]{0:T(128)} %pad_add_fusion.planes_ref.bounds_ref, f32[4]{0:T(128)} %pad_maximum_fusion.waves_ref, f32[2560,128]{1,0:T(8,128)} %bitcast.50, bf16[3,128,128]{2,1,0:T(8,128)(2,1)} %constant.70.clone.y_ref, bf16[3,128,512]{2,1,0:T(8,128)(2,1)} %constant.71.clone.y_back_ref, ...), custom_call_target="tpu_custom_call" | custom-call | tf_op jit(solution)/shard_map/planes/pallas_call | solution.py:620
  135.4 1.0 copy-done.3
  136.5 2.7 %all-to-all-start.1 = ((f32[32,80,128]{2,1,0:T(8,128)}), f32[32,80,128]{2,1,0:T(8,128)S(1)}, u32[]{:S(2)}, u32[]{:S(2)}) async-start(f32[32,80,128]{2,1,0:T(8,128)} %bitcast.53), calls=%async_computation.1 | async-start | bytes 2621440 | tf_op jit(solution)/shard_map/all_to_all | solution.py:509
  139.2 0.6 pad_add_fusion.1.planes_ref.bounds_ref
  139.8 36.6 %kernel_table.3.table_hbm = f32[2,160,72,128]{3,2,1,0:T(8,128)} custom-call(s32[3]{0:T(128)} %pad_add_fusion.1.planes_ref.bounds_ref, s32[3]{0:T(128)} %pad_add_fusion.1.planes_ref.bounds_ref, f32[8,160,128]{2,1,0:T(8,128)} %get-tuple-element.14.value_ref, f32[8,160,128]{2,1,0:T(8,128)} %get-tuple-element.13.step_ref), custom_call_target="tpu_custom_call" | custom-call | tf_op jit(solution)/shard_map/kernel_table/pallas_call | solution.py:586
  177.0 11.8 %planes.3 = (f32[2560,128]{1,0:T(8,128)}, f32[8,128]{1,0:T(8,128)}) custom-call(s32[3]{0:T(128)} %pad_add_fusion.1.planes_ref.bounds_ref, f32[4]{0:T(128)} %pad_maximum_fusion.1.waves_ref, f32[2560,128]{1,0:T(8,128)} %bitcast.49, bf16[3,128,128]{2,1,0:T(8,128)(2,1)} %constant.70.clone.y_ref, bf16[3,128,512]{2,1,0:T(8,128)(2,1)} %constant.71.clone.y_back_ref, ...), custom_call_target="tpu_custom_call" | custom-call | tf_op jit(solution)/shard_map/planes/pallas_call | solution.py:620
  188.8 1.0 copy-done.1
  189.9 5.8 %all-to-all-start.3 = ((f32[32,80,128]{2,1,0:T(8,128)}), f32[32,80,128]{2,1,0:T(8,128)S(1)}, u32[]{:S(2)}, u32[]{:S(2)}) async-start(f32[32,80,128]{2,1,0:T(8,128)} %bitcast.52), calls=%async_computation.3 | async-start | bytes 2621440 | tf_op jit(solution)/shard_map/all_to_all | solution.py:509
  195.7 1.8 collective-permute-start
  197.6 20.1 %collective-permute-done = f32[8,128]{1,0:T(8,128)S(1)} collective-permute-done((f32[8,128]{1,0:T(8,128)S(1)}, f32[8,128]{1,0:T(8,128)S(1)}, u32[]{:S(2)}, u32[]{:S(2)}) %collective-permute-start) | collective-permute-done | bytes 4128 | tf_op jit(solution)/shard_map/ppermute | solution.py:502
  217.7 4.4 %collective-permute-start.1 = (f32[8,128]{1,0:T(8,128)S(1)}, f32[8,128]{1,0:T(8,128)S(1)}, u32[]{:S(2)}, u32[]{:S(2)}) collective-permute-start(f32[8,128]{1,0:T(8,128)S(1)} %add.42), channel_id=1, source_target_pairs={{0,2},{1,3},{2,0},{3,1},{4,6},{5,7},{6,4},{7,5},{8,10},{9,11},{10,... | collective-permute-start | bytes 12296 | tf_op jit(solution)/shard_map/ppermute | solution.py:502
  222.1 5.6 %collective-permute-done.1 = f32[8,128]{1,0:T(8,128)S(1)} collective-permute-done((f32[8,128]{1,0:T(8,128)S(1)}, f32[8,128]{1,0:T(8,128)S(1)}, u32[]{:S(2)}, u32[]{:S(2)}) %collective-permute-start.1) | collective-permute-done | bytes 4128 | tf_op jit(solution)/shard_map/ppermute | solution.py:502
  227.7 1.2 collective-permute-done.2
  228.9 1.5 collective-permute-start.3
  230.4 2.1 collective-permute-done.3
  232.5 1.5 collective-permute-start.4
  234.0 2.1 collective-permute-done.4
  236.3 0.7 gather_fusion.2
  237.0 0.7 reshape.59
  237.7 1.0 copy-done.2
  238.7 7.2 %z_inverse.1 = f32[10,512,128]{2,1,0:T(8,128)} custom-call(f32[2560,128]{1,0:T(8,128)} %bitcast.47, f32[2560,128]{1,0:T(8,128)} %bitcast.48, bf16[384,128]{1,0:T(8,128)(2,1)} %constant.72.clone.refs_2_), custom_call_target="tpu_custom_call" | custom-call | tf_op jit(solution)/shard_map/z_inverse/pallas_call | solution.py:645
  (37 shorter events, 1.8 us)
Async XLA Ops:
  0.6 51.1 %copy-start = (f32[1024,100]{0,1:T(8,128)S(1)}, f32[1024,100]{0,1:T(8,128)}, u32[]{:S(2)}) copy-start(f32[1024,100]{0,1:T(8,128)} %param.18) | copy-start | bytes 1228804
  8.3 37.7 %all-to-all-start = ((f32[32,80,128]{2,1,0:T(8,128)}), f32[32,80,128]{2,1,0:T(8,128)S(1)}, u32[]{:S(2)}, u32[]{:S(2)}) async-start(f32[32,80,128]{2,1,0:T(8,128)} %bitcast.46), calls=%async_computation | async-start | bytes 2621440 | tf_op jit(solution)/shard_map/all_to_all | solution.py:509
  46.0 1.1 copy-start.4
  46.0 5.7 %copy-start.10 = (s32[55]{0:T(128)S(1)}, s32[55]{0:T(128)}, u32[]{:S(2)}) copy-start(s32[55]{0:T(128)} %constant.81) | copy-start | bytes 664
  47.0 88.4 %all-to-all-start.2 = ((f32[32,80,128]{2,1,0:T(8,128)}), f32[32,80,128]{2,1,0:T(8,128)S(1)}, u32[]{:S(2)}, u32[]{:S(2)}) async-start(f32[32,80,128]{2,1,0:T(8,128)} %bitcast.45), calls=%async_computation.2 | async-start | bytes 2621440 | tf_op jit(solution)/shard_map/all_to_all | solution.py:509
  51.7 0.7 copy-start.9
  52.4 1.3 copy-start.5
  135.4 1.1 copy-start.3
  136.5 52.3 %all-to-all-start.1 = ((f32[32,80,128]{2,1,0:T(8,128)}), f32[32,80,128]{2,1,0:T(8,128)S(1)}, u32[]{:S(2)}, u32[]{:S(2)}) async-start(f32[32,80,128]{2,1,0:T(8,128)} %bitcast.53), calls=%async_computation.1 | async-start | bytes 2621440 | tf_op jit(solution)/shard_map/all_to_all | solution.py:509
  188.8 1.1 copy-start.1
  188.8 6.9 %copy-start.6 = (f32[8,128]{1,0:T(8,128)S(1)}, f32[8,128]{1,0:T(8,128)}, u32[]{:S(2)}) copy-start(f32[8,128]{1,0:T(8,128)} %get-tuple-element.9) | copy-start | bytes 12292
  188.8 6.9 %copy-start.7 = (f32[8,128]{1,0:T(8,128)S(1)}, f32[8,128]{1,0:T(8,128)}, u32[]{:S(2)}) copy-start(f32[8,128]{1,0:T(8,128)} %get-tuple-element.10) | copy-start | bytes 12292
  188.8 45.1 %copy-start.8 = (s32[9]{0:T(128)S(1)}, s32[9]{0:T(128)}, u32[]{:S(2)}) copy-start(s32[9]{0:T(128)} %constant.83) | copy-start | bytes 112
  189.9 47.8 %all-to-all-start.3 = ((f32[32,80,128]{2,1,0:T(8,128)}), f32[32,80,128]{2,1,0:T(8,128)S(1)}, u32[]{:S(2)}, u32[]{:S(2)}) async-start(f32[32,80,128]{2,1,0:T(8,128)} %bitcast.52), calls=%async_computation.3 | async-start | bytes 2621440 | tf_op jit(solution)/shard_map/all_to_all | solution.py:509
  195.7 22.0 %collective-permute-start = (f32[8,128]{1,0:T(8,128)S(1)}, f32[8,128]{1,0:T(8,128)S(1)}, u32[]{:S(2)}, u32[]{:S(2)}) collective-permute-start(f32[8,128]{1,0:T(8,128)S(1)} %add.41), channel_id=1, source_target_pairs={{0,1},{1,0},{2,3},{3,2},{4,5},{5,4},{6,7},{7,6},{8,9},{9,8},{10,11... | collective-permute-start | bytes 12296 | tf_op jit(solution)/shard_map/ppermute | solution.py:502
  217.7 10.0 %collective-permute-start.1 = (f32[8,128]{1,0:T(8,128)S(1)}, f32[8,128]{1,0:T(8,128)S(1)}, u32[]{:S(2)}, u32[]{:S(2)}) collective-permute-start(f32[8,128]{1,0:T(8,128)S(1)} %add.42), channel_id=1, source_target_pairs={{0,2},{1,3},{2,0},{3,1},{4,6},{5,7},{6,4},{7,5},{8,10},{9,11},{10,... | collective-permute-start | bytes 12296 | tf_op jit(solution)/shard_map/ppermute | solution.py:502
  227.7 1.2 collective-permute-start.2
  228.9 3.6 %collective-permute-start.3 = (f32[8,128]{1,0:T(8,128)S(1)}, f32[8,128]{1,0:T(8,128)S(1)}, u32[]{:S(2)}, u32[]{:S(2)}) collective-permute-start(f32[8,128]{1,0:T(8,128)S(1)} %add.44), channel_id=1, source_target_pairs={{0,8},{1,9},{2,10},{3,11},{4,12},{5,13},{6,14},{7,15},{8,0},{9,1},... | collective-permute-start | bytes 12296 | tf_op jit(solution)/shard_map/ppermute | solution.py:502
  232.5 3.6 %collective-permute-start.4 = (f32[8,128]{1,0:T(8,128)S(1)}, f32[8,128]{1,0:T(8,128)S(1)}, u32[]{:S(2)}, u32[]{:S(2)}) collective-permute-start(f32[8,128]{1,0:T(8,128)S(1)} %add.45), channel_id=1, source_target_pairs={{0,16},{1,17},{2,18},{3,19},{4,20},{5,21},{6,22},{7,23},{8,24},{9,... | collective-permute-start | bytes 12296 | tf_op jit(solution)/shard_map/ppermute | solution.py:502
  237.7 1.1 copy-start.2

commit v2 on v1

--- a/solution.py
+++ b/solution.py
@@ -8,6 +8,7 @@
 from jax.experimental import pallas as pl
 from jax.experimental.pallas import tpu as pltpu
 from jax.sharding import PartitionSpec as P
+
 
 HIGHEST = lax.Precision.HIGHEST
 TWO_PI = 2.0 * math.pi
@@ -198,7 +199,10 @@
 LANES = 128
 SUBLANES = 8
 STATS = 7
+HALF_BITS = 16
+MIDDLE = 1 << 15
 AXES = ("gx", "gy")
+WHOLE = 60 << 20
 
 
 def real_basis(length):
@@ -235,48 +239,85 @@
     )
 
 
-def z_forward_kernel(theta_ref, basis_ref, out_ref, *, q_count, groups, devices, rows):
-    q = pl.program_id(0)
-    high, low = split(theta_ref[0])
-    spectrum = product(basis_ref[...], jnp.concatenate([high, low, high], axis=1), 1)
-    for j in range(2):
+def z_forward_kernel(theta_ref, basis_ref, out_ref, *, q_count, block, groups, devices, rows):
+    basis = basis_ref[...]
+    for k in range(block):
+        high, low = split(theta_ref[k])
+        spectrum = product(basis, jnp.concatenate([high, low, high], axis=1), 1)
+        q = pl.program_id(0) * block + k
+        for j in range(2):
+            for g in range(groups):
+                out_ref[pl.ds((g * 2 + j) * q_count + q, devices, stride=rows), :] = spectrum[
+                    j * devices : (j + 1) * devices, g * LANES : (g + 1) * LANES
+                ]
+
+
+def pack_kernel(own_ref, near_ref, far_ref, *out_refs, rows):
+    pieces = len(out_refs) // 2
+    for k in range(pieces):
+        block = slice(k * rows, (k + 1) * rows)
+        out_refs[k][0:rows, :] = own_ref[block, :]
+        out_refs[k][rows : 2 * rows, :] = near_ref[block, :]
+        out_refs[k][2 * rows : 3 * rows, :] = far_ref[block, :]
+        out_refs[pieces + k][...] = far_ref[(pieces + k) * rows : (pieces + k + 1) * rows, :]
+
+
+def z_inverse_kernel(*refs, q_count, block, groups, devices, rows, last_rows, direct, gy_size, cell_total):
+    gx_size = devices // gy_size
+    pieces, refs = refs[: 2 * gx_size], refs[2 * gx_size :]
+    direct_refs, refs = refs[:direct], refs[direct:]
+    basis_ref, out_ref, stress_ref, energy_ref, first_ref = refs
+    basis = basis_ref[...]
+
+    @pl.when(pl.program_id(0) == 0)
+    def _():
+        my_x, my_y = lax.axis_index("gx"), lax.axis_index("gy")
+        for k, piece in enumerate(pieces):
+            for b, across in enumerate((0, 1, 2) if k < gx_size else (3,)):
+                source = (my_x ^ (k % gx_size)) * gy_size + (my_y ^ across)
+                first_ref[pl.ds(pl.multiple_of(source * rows, SUBLANES), rows), :] = piece[
+                    b * rows : (b + 1) * rows, :
+                ]
+        last = direct_refs[-1]
+        total = None
+        for d in range(devices):
+            part = last[(d + 1) * last_rows - SUBLANES : (d + 1) * last_rows, :]
+            total = part if total is None else total + part
+        terms = [jnp.sum(total[k : k + 1, :]) for k in range(STATS)]
+        energy_ref[0, 0] = terms[0] * (0.5 / cell_total)
+        for k, term in enumerate((0, 3, 4, 3, 1, 5, 4, 5, 2)):
+            stress_ref[k // 3, k % 3] = terms[term + 1] * (-0.5 / cell_total)
+
+    sources = [(first_ref, rows)] + [(ref, last_rows if ref is direct_refs[-1] else rows) for ref in direct_refs]
+    for k in range(block):
+        q = pl.program_id(0) * block + k
         for g in range(groups):
-            out_ref[pl.ds((g * 2 + j) * q_count + q, devices, stride=rows), :] = spectrum[
-                j * devices : (j + 1) * devices, g * LANES : (g + 1) * LANES
-            ]
-
-
-def z_inverse_kernel(*refs, q_count, groups, devices, rows, slots):
-    sent_refs, basis_ref, out_ref = refs[:slots], refs[slots], refs[slots + 1]
-    q = pl.program_id(0)
-    for g in range(groups):
-        parts = []
-        for sent_ref in sent_refs:
-            for j in range(2):
-                parts.append(
-                    sent_ref[pl.ds((g * 2 + j) * q_count + q, devices, stride=rows), :]
-                )
-        high, low = split(jnp.transpose(jnp.concatenate(parts, axis=0)))
-        out_ref[0, g * LANES : (g + 1) * LANES, :] = product(
-            jnp.concatenate([high, low, high], axis=1), basis_ref[...]
-        )
+            parts = []
+            for sent_ref, stride in sources:
+                for j in range(2):
+                    parts.append(sent_ref[pl.ds((g * 2 + j) * q_count + q, devices, stride=stride), :])
+            high, low = split(jnp.transpose(jnp.concatenate(parts, axis=0)))
+            out_ref[k, g * LANES : (g + 1) * LANES, :] = product(
+                jnp.concatenate([high, low, high], axis=1), basis
+            )
 
 
 def fold(index, half):
     return jnp.where(index > half, index - half, index)
 
 
-def table_kernel(planes_ref, bounds_ref, value_ref, step_ref, out_ref, *, half, pairs, group, scale, tiles, points):
+def device_number():
+    return lax.axis_index("gx") * lax.axis_size("gy") + lax.axis_index("gy")
+
+
+def fill_table(number, bounds_ref, scales_ref, words_ref, out_hbm, table_ref, found_ref, sem, *, half, pairs, scale, points):
     wave = math.pi / half
     row = lax.broadcasted_iota(jnp.int32, (SUBLANES, LANES), 0)
     wave_y = fold(lax.broadcasted_iota(jnp.int32, (SUBLANES, LANES), 1), half).astype(jnp.float32) * wave
+    wave_z = number.astype(jnp.float32) * wave
     blocks = half // SUBLANES + 1
 
-    def one_block(index, _):
-        j = index // blocks
-        block = index % blocks
-        number = planes_ref[j]
-        wave_z = number.astype(jnp.float32) * wave
+    def one_block(block, _):
         last = block == blocks - 1
         along_x = jnp.where(last, jnp.where(row == 0, half, row), row + block * SUBLANES)
         wave_x = along_x.astype(jnp.float32) * wave
@@ -286,56 +327,91 @@
         lower = lower.astype(jnp.int32)
         tile = lower // LANES
         lane = lower % LANES
-        masks = [tile == t for t in range(tiles)]
-        start = pl.multiple_of(block * SUBLANES, SUBLANES)
-
-        def one_group(step, _):
-            for i in range(group):
-                pair = step * group + i
-                value = jnp.zeros((SUBLANES, LANES), jnp.float32)
-                slope = value
-                for t in range(tiles):
-                    def look(ref):
-                        source = jnp.broadcast_to(ref[t, pl.ds(pair, 1), :], (SUBLANES, LANES))
-                        return jnp.take_along_axis(source, lane, axis=1, mode="promise_in_bounds")
-                    value = jnp.where(masks[t], look(value_ref), value)
-                    slope = jnp.where(masks[t], look(step_ref), slope)
-                out_ref[j, pair, pl.ds(start, SUBLANES), :] = value + fraction * slope
+        entry = (number * blocks + block) * 2
+
+        def one_tile(t, _):
+            mine = tile == t
+            for pair in range(pairs):
+                source = jnp.broadcast_to(words_ref[t, pair : pair + 1, :], (SUBLANES, LANES))
+                found = jnp.take_along_axis(source, lane, axis=1, mode="promise_in_bounds")
+                found_ref[pair] = jnp.where(mine, found, found_ref[pair])
             return 0
 
-        lax.fori_loop(0, pairs // group, one_group, 0)
+        lax.fori_loop(bounds_ref[entry], bounds_ref[entry + 1], one_tile, 0)
+        for pair in range(pairs):
+            word = found_ref[pair]
+            below = (word >> HALF_BITS).astype(jnp.float32)
+            above = (word & (2 * MIDDLE - 1)).astype(jnp.float32) - MIDDLE
+            table_ref[block, pair] = (below + fraction * (above - below)) * scales_ref[pair]
+        pltpu.make_async_copy(table_ref.at[block], out_hbm.at[block], sem).start()
         return 0
 
-    lax.fori_loop(0, planes_ref[2] * blocks, one_block, 0)
+    lax.fori_loop(0, blocks, one_block, 0)
+    pltpu.make_async_copy(table_ref, out_hbm, sem).wait()
+
+
+def table_kernel(bounds_ref, scales_ref, words_ref, out_hbm, table_ref, found_ref, sem, *, base, **sizes):
+    fill_table(base + device_number(), bounds_ref, scales_ref, words_ref, out_hbm, table_ref, found_ref, sem, **sizes)
+
+
+def second_table_kernel(bounds_ref, scales_ref, words_ref, out_hbm, table_ref, found_ref, sem, *, base, **sizes):
+    @pl.when(base + device_number() == 0)
+    def _():
+        fill_table(jnp.int32(sizes["half"]), bounds_ref, scales_ref, words_ref, out_hbm, table_ref, found_ref, sem, **sizes)
+
+
+def tile_bounds(half, scale, points):
+    blocks = half // SUBLANES + 1
+    wave = math.pi / half
+    bounds = []
+    for number in range(half + 1):
+        for block in range(blocks):
+            low_x = 1 if block == blocks - 1 else block * SUBLANES
+            high_x = half if block == blocks - 1 else block * SUBLANES + SUBLANES - 1
+            low = math.sqrt(low_x**2 + number**2) * wave * scale - 0.1
+            high = math.sqrt(high_x**2 + half**2 + number**2) * wave * scale + 0.1
+            low, high = (int(min(max(math.floor(r), 0), points - 2)) // LANES for r in (low, high))
+            bounds += [low, high + 1]
+    return np.array(bounds, dtype=np.int32)
+
+
+def mark_kernel(stats_ref, out_ref):
+    out_ref[...] = stats_ref[...]
 
 
 def plane_kernel(
-    planes_ref,
-    waves_ref,
     sent_ref,
     y_ref,
     y_back_ref,
     x_ref,
     x_back_ref,
-    table_hbm,
-    out_ref,
-    stats_ref,
-    table_ref,
-    y_wide_ref,
-    y_back_wide_ref,
-    rows_ref,
-    spectrum_ref,
-    u_ref,
-    sem,
-    *,
+    *rest,
+    base,
     q_count,
     gx_size,
     gy_size,
     rows,
+    out_rows,
     half,
+    n_tables,
+    hopped,
 ):
-    copy = pltpu.make_async_copy(table_hbm, table_ref, sem)
-    copy.start()
+    before, rest = rest[: 1 - hopped], rest[1 - hopped :]
+    tables, rest = rest[:n_tables], rest[n_tables:]
+    my_x, my_y = lax.axis_index("gx"), lax.axis_index("gy")
+    slot = base + device_number()
+    special = slot == 0
+    out_refs, rest = rest[: 1 + 2 * hopped], rest[1 + 2 * hopped :]
+    stats_ref, y_wide_ref, y_back_wide_ref, rows_ref, spectrum_ref, u_ref, tables_ref, sem = rest
+    first_copy = pltpu.make_async_copy(tables[0], tables_ref.at[0], sem.at[0])
+    first_copy.start()
+    if n_tables > 1:
+        second_copy = pltpu.make_async_copy(tables[1], tables_ref.at[1], sem.at[1])
+
+        @pl.when(special)
+        def _():
+            second_copy.start()
+
     full = 2 * half
     local_y = full // gy_size
     spread = LANES // local_y
@@ -361,17 +437,15 @@
                 lane_part == k, y_back_ref[part].astype(jnp.float32), 0.0
             ).astype(bf16)
 
-    for x in range(gx_size):
-        highs, lows = [], []
-        for s in range(gy_size):
-            top = (x * gy_size + s) * rows
-            high, low = split(sent_ref[top : top + rows, :])
-            highs.append(high)
-            lows.append(low)
-        result = product(jnp.concatenate(highs + lows + highs, axis=1), y_wide_ref[...])
-        for k in range(spread):
-            top = k * total_rows + x * rows
-            rows_ref[top : top + rows, :] = result[:, k * full : (k + 1) * full]
+    highs, lows = [], []
+    for s in range(gy_size):
+        tops = [(x * gy_size + s) * rows for x in range(gx_size)]
+        high, low = split(jnp.concatenate([sent_ref[top : top + rows, :] for top in tops], axis=0))
+        highs.append(high)
+        lows.append(low)
+    result = product(jnp.concatenate(highs + lows + highs, axis=1), y_wide_ref[...])
+    for k in range(spread):
+        rows_ref[k * total_rows : (k + 1) * total_rows, :] = result[:, k * full : (k + 1) * full]
 
     for first in range(0, planes, 2):
         pair = []
@@ -390,15 +464,24 @@
         for i in range(2):
             spectrum_ref[(first + i) * full : (first + i + 1) * full, :] = result[:, i * full : (i + 1) * full]
 
-    copy.wait()
+    first_copy.wait()
+    if n_tables > 1:
+
+        @pl.when(special)
+        def _():
+            second_copy.wait()
+
     wave = math.pi / half
     lane = lax.broadcasted_iota(jnp.int32, (SUBLANES, LANES), 1)
     row = lax.broadcasted_iota(jnp.int32, (SUBLANES, LANES), 0)
     wave_y = fold(lane, half).astype(jnp.float32) * wave
     signed_y = jnp.where(lane < half, wave_y, jnp.where(lane == half, 0.0, -wave_y))
     nyquist_y = jnp.where(lane == half, math.pi, 0.0)
-    wave_z0, wave_z1, cross_z, nyquist_z = (waves_ref[i] for i in range(4))
-    plane_index = (0, planes_ref[2] - 1)
+    wave_z0 = slot.astype(jnp.float32) * wave
+    wave_z1 = jnp.where(special, math.pi, wave_z0)
+    cross_z = wave_z0
+    nyquist_z = jnp.where(special, math.pi, 0.0)
+    table_of = (0, jnp.where(special, 1, 0) if n_tables > 1 else 0)
     upper = {}
     for q in range(q_count):
         for p in range(q, q_count):
@@ -410,7 +493,7 @@
     def one_block(block, carry):
         energy, xx, yy, zz, xy, xz, yz = carry
         top = pl.multiple_of(block * SUBLANES, SUBLANES)
-        tops = (top, pl.multiple_of(jnp.where(block == 0, half, top), SUBLANES))
+        tops = (block, jnp.where(block == 0, half // SUBLANES, block))
         values = {}
         for j in range(2):
             for h in range(2):
@@ -427,13 +510,13 @@
                 j, h = key
                 u = None
                 for p in range(q_count):
-                    term = table_ref[plane_index[j], q * q_count + p, pl.ds(tops[h], SUBLANES), :] * values[key][p]
+                    term = tables_ref[table_of[j], tops[h], q * q_count + p] * values[key][p]
                     u = term if u is None else u + term
                 u_ref[pl.ds(pl.multiple_of((j * q_count + q) * full + h * half + top, SUBLANES), SUBLANES), :] = u
                 energy = energy + u * values[key][q]
                 v = None
                 for p in range(q_count):
-                    term = table_ref[plane_index[j], upper[q, p], pl.ds(tops[h], SUBLANES), :] * values[key][p]
+                    term = tables_ref[table_of[j], tops[h], upper[q, p]] * values[key][p]
                     v = term if v is None else v + term
                 bent[key] = v
                 form[key] = form[key] + v * values[key][q]
@@ -454,9 +537,11 @@
 
     start = (jnp.zeros((SUBLANES, LANES), jnp.float32),) * STATS
     sums = lax.fori_loop(0, half // SUBLANES, one_block, start)
-    stats_ref[...] = jnp.concatenate(
+    sums = jnp.concatenate(
         [jnp.sum(part, axis=0, keepdims=True) for part in sums] + [jnp.zeros((1, LANES), jnp.float32)], axis=0
     )
+
+    stats_ref[...] = before[0][...] + sums if before else sums
 
     for first in range(0, planes, 2):
         high, low = split(
@@ -471,13 +556,36 @@
                     k * high_x : (k + 1) * high_x, i * full : (i + 1) * full
                 ]
 
+    strips_of = [split(rows_ref[k * total_rows : (k + 1) * total_rows, :]) for k in range(spread)]
+    highs = [part[0] for part in strips_of]
+    lows = [part[1] for part in strips_of]
+    result = product(jnp.concatenate(highs + lows + highs, axis=1), y_back_wide_ref[...])
+    half_y = gy_size // 2
     for x in range(gx_size):
-        strip = [rows_ref[k * total_rows + x * rows : k * total_rows + (x + 1) * rows, :] for k in range(spread)]
-        high, low = split(jnp.concatenate(strip, axis=1))
-        result = product(jnp.concatenate([high, low, high], axis=1), y_back_wide_ref[...])
         for s in range(gy_size):
-            top = (x * gy_size + s) * rows
-            out_ref[top : top + rows, :] = result[:, s * LANES : (s + 1) * LANES]
+            value = result[x * rows : (x + 1) * rows, s * LANES : (s + 1) * LANES]
+            if hopped:
+                across = my_y ^ s
+                near_top = pl.multiple_of((my_x ^ x) * rows, SUBLANES)
+                far_top = pl.multiple_of(((across % half_y) * gx_size + (my_x ^ x)) * rows, SUBLANES)
+
+                @pl.when(across == 0)
+                def _(value=value, top=near_top):
+                    out_refs[0][pl.ds(top, rows), :] = value
+
+                @pl.when(across == 1)
+                def _(value=value, top=near_top):
+                    out_refs[1][pl.ds(top, rows), :] = value
+
+                @pl.when(across >= half_y)
+                def _(value=value, top=far_top):
+                    out_refs[2][pl.ds(top, rows), :] = value
+
+            else:
+                top = (x * gy_size + s) * out_rows
+                out_refs[0][top : top + rows, :] = value
+                if out_rows > rows:
+                    out_refs[0][top + rows : top + out_rows, :] = stats_ref[...]
 
 
 def table_rows(phi_table, dphi_table, q_count, padded):
@@ -487,21 +595,13 @@
     slopes = dphi_table.T
     slopes = 0.5 * (slopes[first] + slopes[second])
     table = jnp.concatenate([phi_table.T, slopes], axis=0)
-    table = jnp.pad(table, ((0, padded - table.shape[0]), (0, 0)))
-    steps = jnp.pad(table[:, 1:] - table[:, :-1], ((0, 0), (0, 1)))
-
-    def tiled(values):
-        return values.reshape(padded, points // LANES, LANES).transpose(1, 0, 2)
-
-    return tiled(table), tiled(steps)
-
-
-def butterfly(value, devices):
-    step = 1
-    while step < devices:
-        value = value + lax.ppermute(value, AXES, [(i, i ^ step) for i in range(devices)])
-        step *= 2
-    return value
+    top = jnp.max(jnp.abs(table), axis=1)
+    scales = jnp.where(top > 0.0, top, 1.0) / (MIDDLE - 1)
+    steps = jnp.round(table / scales[:, None]).astype(jnp.int32)
+    following = jnp.concatenate([steps[:, 1:], steps[:, -1:]], axis=1)
+    words = steps * (2 * MIDDLE) + (following + MIDDLE)
+    words = jnp.pad(words, ((0, padded - words.shape[0]), (0, 0)))
+    return words.reshape(padded, points // LANES, LANES).transpose(1, 0, 2), scales
 
 
 def swap(value, devices):
@@ -520,12 +620,10 @@
     groups = local_x * local_y // LANES
     spread = LANES // local_y
     rows = groups * 2 * q_count
-    me = lax.axis_index("gx") * gy_size + lax.axis_index("gy")
     table_points = phi_table.shape[0]
-    tiles = table_points // LANES
     upper_pairs = q_count * (q_count + 1) // 2
-    group = 16
-    padded = -(-(q_count * q_count + upper_pairs) // group) * group
+    pairs = q_count * q_count + upper_pairs
+    padded = -(-pairs // SUBLANES) * SUBLANES
     cell_total = full * full * depth
     vmem = pl.BlockSpec(memory_space=pltpu.VMEM)
     smem = pl.BlockSpec(memory_space=pltpu.SMEM)
@@ -538,67 +636,73 @@
         return slot if j == 0 else (depth // 2 + slot)
 
     order = [
-        [coefficient(c * devices + d, j) for j in range(2) for d in range(devices)] for c in range(slots)
+        [coefficient((slots - 1 - c) * devices + d, j) for j in range(2) for d in range(devices)]
+        for c in range(slots)
     ]
     flat_theta = theta.reshape(q_count, local_x * local_y, depth)
-    sent = []
+    block = max(k for k in range(1, 6) if q_count % k == 0)
+    arrived = []
     for c in range(slots):
         high, low = halves(z_basis[order[c]])
-        sent.append(
-            pl.pallas_call(
-                functools.partial(
-                    z_forward_kernel, q_count=q_count, groups=groups, devices=devices, rows=rows
-                ),
-                grid=(q_count,),
-                in_specs=[
-                    pl.BlockSpec((1, local_x * local_y, depth), lambda q: (q, 0, 0)),
-                    pl.BlockSpec((2 * devices, 3 * depth), lambda q: (0, 0)),
-                ],
-                out_specs=pl.BlockSpec((devices * rows, LANES), lambda q: (0, 0)),
-                out_shape=jax.ShapeDtypeStruct((devices * rows, LANES), jnp.float32),
-                name="z_forward",
-            )(flat_theta, jnp.asarray(np.concatenate([high, high, low], axis=1)))
-        )
-    arrived = [swap(part, devices) for part in sent]
-
-    value_table, step_table = table_rows(phi_table, dphi_table, q_count, padded)
-    wave = math.pi / half
+        sent = pl.pallas_call(
+            functools.partial(
+                z_forward_kernel,
+                q_count=q_count,
+                block=block,
+                groups=groups,
+                devices=devices,
+                rows=rows,
+            ),
+            grid=(q_count // block,),
+            in_specs=[
+                pl.BlockSpec((block, local_x * local_y, depth), lambda q: (q, 0, 0)),
+                pl.BlockSpec((2 * devices, 3 * depth), lambda q: (0, 0)),
+            ],
+            out_specs=pl.BlockSpec((devices * rows, LANES), lambda q: (0, 0)),
+            out_shape=jax.ShapeDtypeStruct((devices * rows, LANES), jnp.float32),
+            compiler_params=pltpu.CompilerParams(vmem_limit_bytes=WHOLE),
+            name="z_forward",
+        )(flat_theta, jnp.asarray(np.concatenate([high, high, low], axis=1)))
+        arrived.append(swap(sent, devices))
+
+    words, scales = table_rows(phi_table, dphi_table, q_count, padded)
     scale = (table_points - 1) / (math.pi * math.sqrt(3.0))
-    tables, settings = [], []
+    bounds = jnp.asarray(tile_bounds(half, scale, table_points))
+    tables = []
     blocks = half // SUBLANES + 1
     for c in range(slots):
-        slot = c * devices + me
-        special = slot == 0
-        plane_numbers = jnp.stack(
-            [slot, jnp.where(special, half, slot), jnp.where(special, 2, 1)]
-        ).astype(jnp.int32)
-        number = slot.astype(jnp.float32) * wave
-        wave_values = jnp.stack(
-            [
-                number,
-                jnp.where(special, math.pi, number),
-                jnp.where(special, 0.0, number),
-                jnp.where(special, math.pi, 0.0),
-            ]
-        )
-        settings.append((plane_numbers, wave_values))
-        tables.append(
+        sizes = dict(base=(slots - 1 - c) * devices, half=half, pairs=pairs, scale=scale, points=table_points)
+        table_shape = jax.ShapeDtypeStruct((blocks, pairs, SUBLANES, LANES), jnp.float32)
+        params = pltpu.CompilerParams(vmem_limit_bytes=WHOLE)
+        scratch = [
+            pltpu.VMEM(table_shape.shape, jnp.float32),
+            pltpu.VMEM((pairs, SUBLANES, LANES), jnp.int32),
+            pltpu.SemaphoreType.DMA,
+        ]
+        found = [
             pl.pallas_call(
-                functools.partial(
-                    table_kernel,
-                    half=half,
-                    pairs=padded,
-                    group=group,
-                    scale=scale,
-                    tiles=tiles,
-                    points=table_points,
-                ),
-                in_specs=[smem, smem, vmem, vmem],
-                out_specs=vmem,
-                out_shape=jax.ShapeDtypeStruct((2, padded, blocks * SUBLANES, LANES), jnp.float32),
+                functools.partial(table_kernel, **sizes),
+                in_specs=[smem, smem, vmem],
+                out_specs=hbm,
+                out_shape=table_shape,
+                scratch_shapes=scratch,
+                compiler_params=params,
                 name="kernel_table",
-            )(plane_numbers, plane_numbers, value_table, step_table)
-        )
+            )(bounds, scales, words)
+        ]
+        if c == slots - 1:
+            found.append(
+                pl.pallas_call(
+                    functools.partial(second_table_kernel, **sizes),
+                    in_specs=[smem, smem, vmem],
+                    out_specs=hbm,
+                    out_shape=table_shape,
+                    scratch_shapes=scratch,
+                    compiler_params=params,
+                    name="second_table",
+                )(bounds, scales, words)
+            )
+        tables.append(found)
 
     x_order = [
         (h // groups) * local_x + (h % groups) * spread + k for k in range(spread) for h in range(gx_size * groups)
@@ -615,50 +719,107 @@
         for part in (high, low)
     ]
     y_back = jnp.asarray(np.stack([wide[0], wide[0], wide[1]]))
-    returned, stats = [], None
+    returned = []
+    last_rows = rows + SUBLANES
+    stats = ()
     for c in range(slots):
-        back, part = pl.pallas_call(
+        hopped = c == 0
+        out_rows = last_rows if c == slots - 1 else rows
+        outs = [devices * out_rows]
+        if hopped:
+            outs = [gx_size * rows, gx_size * rows, 2 * gx_size * rows]
+        *back, part = pl.pallas_call(
             functools.partial(
-                plane_kernel, q_count=q_count, gx_size=gx_size, gy_size=gy_size, rows=rows, half=half
+                plane_kernel,
+                q_count=q_count,
+                gx_size=gx_size,
+                gy_size=gy_size,
+                rows=rows,
+                out_rows=out_rows,
+                half=half,
+                base=(slots - 1 - c) * devices,
+                n_tables=len(tables[c]),
+                hopped=hopped,
             ),
-            in_specs=[smem, smem, vmem, vmem, vmem, vmem, vmem, hbm],
-            out_specs=(vmem, vmem),
-            out_shape=(
-                jax.ShapeDtypeStruct((devices * rows, LANES), jnp.float32),
-                jax.ShapeDtypeStruct((SUBLANES, LANES), jnp.float32),
-            ),
+            in_specs=[vmem] * (5 + len(stats)) + [hbm] * len(tables[c]),
+            out_specs=(vmem,) * (len(outs) + 1),
+            out_shape=tuple(jax.ShapeDtypeStruct((count, LANES), jnp.float32) for count in outs)
+            + (jax.ShapeDtypeStruct((SUBLANES, LANES), jnp.float32),),
             scratch_shapes=[
-                pltpu.VMEM((2, padded, blocks * SUBLANES, LANES), jnp.float32),
                 pltpu.VMEM((3 * gy_size * LANES, spread * full), jnp.bfloat16),
                 pltpu.VMEM((3 * spread * full, gy_size * LANES), jnp.bfloat16),
                 pltpu.VMEM((spread * gx_size * rows, full), jnp.float32),
                 pltpu.VMEM((2 * q_count * full, LANES), jnp.float32),
                 pltpu.VMEM((2 * q_count * full, LANES), jnp.float32),
-                pltpu.SemaphoreType.DMA,
+                pltpu.VMEM((len(tables[c]), blocks, pairs, SUBLANES, LANES), jnp.float32),
+                pltpu.SemaphoreType.DMA((len(tables[c]),)),
             ],
+            compiler_params=pltpu.CompilerParams(vmem_limit_bytes=WHOLE),
             name="planes",
-        )(*settings[c], arrived[c], y_forward, y_back, x_forward, x_back, tables[c])
-        returned.append(swap(back, devices))
-        stats = part if stats is None else stats + part
+        )(arrived[c], y_forward, y_back, x_forward, x_back, *stats, *tables[c])
+        if hopped:
+            def hop(value, step):
+                return lax.ppermute(value, AXES, [(d, d ^ step) for d in range(devices)])
+
+            far = hop(back[2], 2)
+            near = hop(back[1], 1)
+            gathered = pl.pallas_call(
+                functools.partial(pack_kernel, rows=rows),
+                in_specs=[vmem] * 3,
+                out_specs=(vmem,) * (2 * gx_size),
+                out_shape=(jax.ShapeDtypeStruct((3 * rows, LANES), jnp.float32),) * gx_size
+                + (jax.ShapeDtypeStruct((rows, LANES), jnp.float32),) * gx_size,
+                compiler_params=pltpu.CompilerParams(vmem_limit_bytes=WHOLE),
+                name="pack",
+            )(back[0], near, far)
+            gathered = list(gathered)
+            for k in [*range(gx_size, 2 * gx_size), *range(1, gx_size)]:
+                gathered[k] = hop(gathered[k], k % gx_size * gy_size + k // gx_size)
+            stats = (
+                pl.pallas_call(
+                    mark_kernel,
+                    in_specs=[vmem],
+                    out_specs=vmem,
+                    out_shape=jax.ShapeDtypeStruct((SUBLANES, LANES), jnp.float32),
+                    name="mark",
+                )(part),
+            )
+        else:
+            returned.append(swap(back[0], devices))
 
     high, low = halves(np.concatenate([z_basis[rows_of] for rows_of in order], axis=0))
-    u_grids = pl.pallas_call(
+    block = max(k for k in range(1, 6) if q_count % k == 0)
+    u_grids, stress, energy = pl.pallas_call(
         functools.partial(
-            z_inverse_kernel, q_count=q_count, groups=groups, devices=devices, rows=rows, slots=slots
+            z_inverse_kernel,
+            q_count=q_count,
+            block=block,
+            groups=groups,
+            devices=devices,
+            rows=rows,
+            last_rows=last_rows,
+            direct=len(returned),
+            gy_size=gy_size,
+            cell_total=cell_total,
         ),
-        grid=(q_count,),
-        in_specs=[pl.BlockSpec((devices * rows, LANES), lambda q: (0, 0))] * slots
+        grid=(q_count // block,),
+        in_specs=[pl.BlockSpec(part.shape, lambda q: (0, 0)) for part in gathered + returned]
         + [pl.BlockSpec((3 * depth, depth), lambda q: (0, 0))],
-        out_specs=pl.BlockSpec((1, local_x * local_y, depth), lambda q: (q, 0, 0)),
-        out_shape=jax.ShapeDtypeStruct((q_count, local_x * local_y, depth), jnp.float32),
+        out_specs=(
+            pl.BlockSpec((block, local_x * local_y, depth), lambda q: (q, 0, 0)),
+            smem,
+            smem,
+        ),
+        out_shape=(
+            jax.ShapeDtypeStruct((q_count, local_x * local_y, depth), jnp.float32),
+            jax.ShapeDtypeStruct((3, 3), jnp.float32),
+            jax.ShapeDtypeStruct((1, 1), jnp.float32),
+        ),
+        scratch_shapes=[pltpu.VMEM((devices * rows, LANES), jnp.float32)],
+        compiler_params=pltpu.CompilerParams(vmem_limit_bytes=WHOLE),
         name="z_inverse",
-    )(*returned, jnp.asarray(np.concatenate([high, high, low], axis=0)))
-
-    totals = jnp.sum(butterfly(stats, devices), axis=1)
-    energy = totals[0] * (0.5 / cell_total)
-    stress_terms = totals[1:STATS] * (-0.5 / cell_total)
-    stress = stress_terms[np.array([0, 3, 4, 3, 1, 5, 4, 5, 2])].reshape(3, 3)
-    return (u_grids.reshape(theta.shape), stress, energy)
+    )(*gathered, *returned, jnp.asarray(np.concatenate([high, high, low], axis=0)))
+    return (u_grids.reshape(theta.shape), stress, energy.reshape(()))
 
 
 def shards(theta, phi_table, dphi_table):
@@ -670,13 +831,16 @@
         local_x * gx_size == LANES
         and local_y * gy_size == LANES
         and depth == LANES
-        and depth % (2 * devices) == 0
+        and depth == 4 * devices
+        and gy_size == 4
         and local_x * local_y % LANES == 0
         and phi_table.shape[0] % LANES == 0
         and devices & (devices - 1) == 0
         and (local_x * local_y // LANES) * q_count % 4 == 0
     )
-    return (real_shards if fits else general_shards)(theta, phi_table, dphi_table)
+    if not fits:
+        return general_shards(theta, phi_table, dphi_table)
+    return real_shards(theta, phi_table, dphi_table)
 
 
 def solution(mesh):

time: 248 us -> 213 us (0.86)
  Pallas kernels: 150 us -> 73.2 us
  waiting for transfers between devices: 53.9 us -> 99 us
  starting transfers between devices: 29.7 us -> 33.4 us
  local copies, waits for them, and re-layouts: 8.09 us -> 4.87 us
  other arithmetic: 2.98 us -> 0.48 us
    pallas_call x5 -> x8, Pallas kernels: 127 us -> 52.6 us  [the longest x2 25.8 us: real_shards(): pl.pallas_call(functools.partial(table_kernel, **sizes), in_specs=[smem,...]
    ppermute x5 -> x17, waiting for transfers between devices: 31.1 us -> 72.6 us  [hop(): return lax.ppermute(value, AXES, [(d, d ^ step) for d in range(devices)])]
    ppermute x5 -> x17, starting transfers between devices: 9.19 us -> 18.4 us  [hop(): return lax.ppermute(value, AXES, [(d, d ^ step) for d in range(devices)])]
    all_to_all x4 -> x3, starting transfers between devices: 20.5 us -> 15.1 us  [swap(): lax.all_to_all(parts, AXES, split_axis=0, concat_axis=0, tiled=True)]
    all_to_all x4 -> x3, waiting for transfers between devices: 22.8 us -> 26.4 us  [swap(): lax.all_to_all(parts, AXES, split_axis=0, concat_axis=0, tiled=True)]
    pallas_call x2, Pallas kernels: 23.7 us -> 20.6 us  [real_shards(): pl.pallas_call(functools.partial(plane_kernel, q_count=q_count, gx_size=g...]
  transfers between devices with their start and end apart: 9 -> 20, of which waited for: 6 -> 10; matrix products, arithmetic and copies ran while one was open for 3% -> 1% of each run, Pallas kernels for 55% -> 25%
where the time goes in v2:
time: 213 us; the launch traced here: 212 us
  waiting for transfers between devices  99 us (46%)
  Pallas kernels  73.2 us (34%)
  starting transfers between devices  33.4 us (16%)
  local copies, waits for them, and re-layouts  4.87 us (2%)
    ppermute x17, waiting for transfers between devices, hop(): return lax.ppermute(value, AXES, [(d, d ^ step) for d in range(devices)])  72.6 us
    all_to_all x3, waiting for transfers between devices, swap(): lax.all_to_all(parts, AXES, split_axis=0, concat_axis=0, tiled=True)  26.4 us
    pallas_call x2, Pallas kernels, real_shards(): pl.pallas_call(functools.partial(table_kernel, **sizes), in_specs=[smem,...  25.8 us
    pallas_call x2, Pallas kernels, real_shards(): pl.pallas_call(functools.partial(plane_kernel, q_count=q_count, gx_size=g...  20.6 us
    ppermute x17, starting transfers between devices, hop(): return lax.ppermute(value, AXES, [(d, d ^ step) for d in range(devices)])  18.4 us
    all_to_all x3, starting transfers between devices, swap(): lax.all_to_all(parts, AXES, split_axis=0, concat_axis=0, tiled=True)  15.1 us
    pallas_call x1, Pallas kernels, real_shards(): pl.pallas_call(functools.partial(second_table_kernel, **sizes), in_specs=...  10.4 us
    pallas_call x2, Pallas kernels, real_shards(): pl.pallas_call(functools.partial(z_forward_kernel, q_count=q_count, block...  7.98 us
  transfers between devices with their start and end apart: 20, of which 10 were waited for; matrix products, arithmetic and copies ran while one was open for 1% of the time, Pallas kernels for 25%

profile of v2, /device:TPU:0, one launch (start us, length us, event | category | flops | bytes accessed | tf_op | source)
XLA Modules:
  0.0 212.0 jit_solution(3947145371577482704)
XLA Ops:
  0.6 4.0 %z_forward.2 = f32[2560,128]{1,0:T(8,128)} custom-call(f32[10,512,128]{2,1,0:T(8,128)} %bitcast.20, bf16[64,384]{1,0:T(8,128)(2,1)} %constant.41.clone.basis_ref), custom_call_target="tpu_custom_call" | custom-call | tf_op jit(solution)/shard_map/z_forward/pallas_call | solution.py:647
  4.6 7.3 %all-to-all-start = ((f32[32,80,128]{2,1,0:T(8,128)}), f32[32,80,128]{2,1,0:T(8,128)S(1)}, u32[]{:S(2)}, u32[]{:S(2)}) async-start(f32[32,80,128]{2,1,0:T(8,128)} %bitcast.24), calls=%async_computation | async-start | bytes 2621440 | tf_op jit(solution)/shard_map/all_to_all | solution.py:609
  12.0 4.0 %z_forward.3 = f32[2560,128]{1,0:T(8,128)} custom-call(f32[10,512,128]{2,1,0:T(8,128)} %bitcast.21, bf16[64,384]{1,0:T(8,128)(2,1)} %constant.42.clone.basis_ref), custom_call_target="tpu_custom_call" | custom-call | tf_op jit(solution)/shard_map/z_forward/pallas_call | solution.py:647
  16.0 26.4 %all-to-all-done = f32[32,80,128]{2,1,0:T(8,128)S(1)} async-done(((f32[32,80,128]{2,1,0:T(8,128)}), f32[32,80,128]{2,1,0:T(8,128)S(1)}, u32[]{:S(2)}, u32[]{:S(2)}) %all-to-all-start) | async-done | bytes 1310752 | tf_op jit(solution)/shard_map/all_to_all | solution.py:609
  42.3 4.8 %all-to-all-start.1 = ((f32[32,80,128]{2,1,0:T(8,128)}), f32[32,80,128]{2,1,0:T(8,128)}, u32[]{:S(2)}, u32[]{:S(2)}) async-start(f32[32,80,128]{2,1,0:T(8,128)} %bitcast.23), calls=%async_computation.1 | async-start | bytes 2621440 | tf_op jit(solution)/shard_map/all_to_all | solution.py:609
  49.7 0.9 bitcast_bitcast_fusion.words_ref
  50.5 12.1 %kernel_table.2.rest_0_ = f32[9,155,8,128]{3,2,1,0:T(8,128)} custom-call(s32[1170]{0:T(1024)} %constant.46.clone.bounds_ref, f32[155]{0:T(256)} %copy-done.21, s32[8,160,128]{2,1,0:T(8,128)} %bitcast_bitcast_fusion.words_ref), custom_call_target="tpu_custom_call" | custom-call | tf_op jit(solution)/shard_map/kernel_table/pallas_call | solution.py:683
  62.6 13.7 %kernel_table.3.rest_1_ = f32[9,155,8,128]{3,2,1,0:T(8,128)} custom-call(s32[1170]{0:T(1024)} %constant.46.clone.bounds_ref, f32[155]{0:T(256)} %copy-done.21, s32[8,160,128]{2,1,0:T(8,128)} %bitcast_bitcast_fusion.words_ref), custom_call_target="tpu_custom_call" | custom-call | tf_op jit(solution)/shard_map/kernel_table/pallas_call | solution.py:683
  76.3 10.4 %second_table.1.rest_2_ = f32[9,155,8,128]{3,2,1,0:T(8,128)} custom-call(s32[1170]{0:T(1024)} %constant.46.clone.bounds_ref, f32[155]{0:T(256)} %copy-done.21, s32[8,160,128]{2,1,0:T(8,128)} %bitcast_bitcast_fusion.words_ref), custom_call_target="tpu_custom_call" | custom-call | tf_op jit(solution)/shard_map/second_table/pallas_call | solution.py:695
  86.8 9.5 %planes.2 = (f32[640,128]{1,0:T(8,128)}, f32[640,128]{1,0:T(8,128)}, f32[1280,128]{1,0:T(8,128)}, f32[8,128]{1,0:T(8,128)}) custom-call(f32[2560,128]{1,0:T(8,128)} %bitcast.25, bf16[3,128,128]{2,1,0:T(8,128)(2,1)} %constant.49.clone.y_ref, bf16[3,128,512]{2,1,0:T(8,128)(2,1)} %constant.50.clone.y_back_ref, bf16[128,384]{1,0:T(8,128)(2,1)} %constant.47.clone.x_ref, ...), custom_call_target="tpu_custom_call" | custom-call | tf_op jit(solution)/shard_map/planes/pallas_call | solution.py:731
  96.3 1.3 mark.1.rest_0_
  97.6 11.1 %planes.3 = (f32[2816,128]{1,0:T(8,128)}, f32[8,128]{1,0:T(8,128)}) custom-call(f32[2560,128]{1,0:T(8,128)} %bitcast.7.sent_ref, bf16[3,128,128]{2,1,0:T(8,128)(2,1)} %constant.49.clone.y_ref, bf16[3,128,512]{2,1,0:T(8,128)(2,1)} %constant.50.clone.y_back_ref, bf16[128,384]{1,0:T(8,128)(2,1)} %constant.47.clone.x_ref, ...), custom_call_target="tpu_custom_call" | custom-call | tf_op jit(solution)/shard_map/planes/pallas_call | solution.py:731
  108.7 3.0 %all-to-all-start.2 = ((f32[32,88,128]{2,1,0:T(8,128)}), f32[32,88,128]{2,1,0:T(8,128)S(1)}, u32[]{:S(2)}, u32[]{:S(2)}) async-start(f32[32,88,128]{2,1,0:T(8,128)} %bitcast.28), calls=%async_computation.2 | async-start | bytes 2883584 | tf_op jit(solution)/shard_map/all_to_all | solution.py:609
  111.7 2.5 %collective-permute-start.1 = (f32[1280,128]{1,0:T(8,128)S(1)}, f32[1280,128]{1,0:T(8,128)S(1)}, u32[]{:S(2)}, u32[]{:S(2)}) collective-permute-start(f32[1280,128]{1,0:T(8,128)S(1)} %copy-done.24), channel_id=1, source_target_pairs={{0,2},{1,3},{2,0},{3,1},{4,6},{5,7},{6,4},{7,5},{8,10},{9,11},{10,... | collective-permute-start | bytes 1966088 | tf_op jit(solution)/shard_map/ppermute | solution.py:762
  114.3 1.5 collective-permute-start
  115.8 40.6 %collective-permute-done.near_ref = f32[640,128]{1,0:T(8,128)S(1)} collective-permute-done((f32[640,128]{1,0:T(8,128)S(1)}, f32[640,128]{1,0:T(8,128)S(1)}, u32[]{:S(2)}, u32[]{:S(2)}) %collective-permute-start) | collective-permute-done | bytes 327712 | tf_op jit(solution)/shard_map/ppermute | solution.py:762
  156.4 17.9 %collective-permute-done.1.far_ref = f32[1280,128]{1,0:T(8,128)S(1)} collective-permute-done((f32[1280,128]{1,0:T(8,128)S(1)}, f32[1280,128]{1,0:T(8,128)S(1)}, u32[]{:S(2)}, u32[]{:S(2)}) %collective-permute-start.1) | collective-permute-done | bytes 655392 | tf_op jit(solution)/shard_map/ppermute | solution.py:762
  174.3 0.9 copy-done.4
  175.1 2.4 %pack.1 = (f32[240,128]{1,0:T(8,128)}, f32[240,128]{1,0:T(8,128)}, f32[240,128]{1,0:T(8,128)}, f32[240,128]{1,0:T(8,128)}, f32[240,128]{1,0:T(8,128)}, /*index=5...) custom-call(f32[640,128]{1,0:T(8,128)} %get-tuple-element.27.own_ref, ...), custom_call_target="tpu_custom_call" | custom-call | tf_op jit(solution)/shard_map/pack/pallas_call | solution.py:766
  177.6 0.9 collective-permute-start.10
  178.5 1.2 collective-permute-start.2
  179.7 1.5 collective-permute-start.3
  181.8 1.4 collective-permute-start.12
  183.2 1.3 collective-permute-start.13
  184.5 2.2 %collective-permute-done.11.refs_10_ = f32[80,128]{1,0:T(8,128)S(1)} collective-permute-done((f32[80,128]{1,0:T(8,128)}, f32[80,128]{1,0:T(8,128)S(1)}, u32[]{:S(2)}, u32[]{:S(2)}) %collective-permute-start.11) | collective-permute-done | bytes 40992 | tf_op jit(solution)/shard_map/ppermute | solution.py:762
  186.8 3.3 %collective-permute-start.15 = (f32[80,128]{1,0:T(8,128)}, f32[80,128]{1,0:T(8,128)S(1)}, u32[]{:S(2)}, u32[]{:S(2)}) collective-permute-start(f32[80,128]{1,0:T(8,128)} %get-tuple-element.44), channel_id=1, source_target_pairs={{0,25},{1,24},{2,27},{3,26},{4,29},{5,28},{6,31},{7,30},{8,17},{9,... | collective-permute-start | bytes 122888 | tf_op jit(solution)/shard_map/ppermute | solution.py:762
  191.4 1.5 collective-permute-done.15.refs_14_
  192.9 1.4 collective-permute-start.5
  194.3 1.2 collective-permute-done.16.refs_15_
  195.7 2.0 collective-permute-start.7
  198.1 7.9 %collective-permute-done.6.refs_5_ = f32[240,128]{1,0:T(8,128)S(1)} collective-permute-done((f32[240,128]{1,0:T(8,128)}, f32[240,128]{1,0:T(8,128)S(1)}, u32[]{:S(2)}, u32[]{:S(2)}) %collective-permute-start.6) | collective-permute-done | bytes 122912 | tf_op jit(solution)/shard_map/ppermute | solution.py:762
  207.3 4.7 %z_inverse.1 = (f32[10,512,128]{2,1,0:T(8,128)}, f32[3,3]{1,0:T(4,128)}, f32[1,1]{1,0:T(1,128)}) custom-call(f32[240,128]{1,0:T(8,128)} %get-tuple-element.30.refs_0_, f32[240,128]{1,0:T(8,128)} %copy-done.6, f32[240,128]{1,0:T(8,128)} %copy-done.7, f32[240,128]{1,0:T(8,128)} %copy-done.8, f32[240,128]{1,0:T(8,128)} %copy-done.9, f32[240,128]{1,0:T(8,128)} %copy-done.10, ...), custom_call_target="tpu_custom_call" | custom-call | tf_op jit(solution)/shard_map/z_inverse/pallas_call | solution.py:792
  (82 shorter events, 6.3 us)
Async XLA Ops:
  0.6 46.5 %copy-start = (f32[1024,100]{0,1:T(8,128)S(1)}, f32[1024,100]{0,1:T(8,128)}, u32[]{:S(2)}) copy-start(f32[1024,100]{0,1:T(8,128)} %param.17) | copy-start | bytes 1228804
  4.6 37.7 %all-to-all-start = ((f32[32,80,128]{2,1,0:T(8,128)}), f32[32,80,128]{2,1,0:T(8,128)S(1)}, u32[]{:S(2)}, u32[]{:S(2)}) async-start(f32[32,80,128]{2,1,0:T(8,128)} %bitcast.24), calls=%async_computation | async-start | bytes 2621440 | tf_op jit(solution)/shard_map/all_to_all | solution.py:609
  16.0 31.2 %copy-start.23 = (s32[55]{0:T(128)S(1)}, s32[55]{0:T(128)}, u32[]{:S(2)}) copy-start(s32[55]{0:T(128)} %constant.56) | copy-start | bytes 664
  42.3 55.2 %all-to-all-start.1 = ((f32[32,80,128]{2,1,0:T(8,128)}), f32[32,80,128]{2,1,0:T(8,128)}, u32[]{:S(2)}, u32[]{:S(2)}) async-start(f32[32,80,128]{2,1,0:T(8,128)} %bitcast.23), calls=%async_computation.1 | async-start | bytes 2621440 | tf_op jit(solution)/shard_map/all_to_all | solution.py:609
  108.7 97.4 %all-to-all-start.2 = ((f32[32,88,128]{2,1,0:T(8,128)}), f32[32,88,128]{2,1,0:T(8,128)S(1)}, u32[]{:S(2)}, u32[]{:S(2)}) async-start(f32[32,88,128]{2,1,0:T(8,128)} %bitcast.28), calls=%async_computation.2 | async-start | bytes 2883584 | tf_op jit(solution)/shard_map/all_to_all | solution.py:609
  111.7 62.5 %collective-permute-start.1 = (f32[1280,128]{1,0:T(8,128)S(1)}, f32[1280,128]{1,0:T(8,128)S(1)}, u32[]{:S(2)}, u32[]{:S(2)}) collective-permute-start(f32[1280,128]{1,0:T(8,128)S(1)} %copy-done.24), channel_id=1, source_target_pairs={{0,2},{1,3},{2,0},{3,1},{4,6},{5,7},{6,4},{7,5},{8,10},{9,11},{10,... | collective-permute-start | bytes 1966088 | tf_op jit(solution)/shard_map/ppermute | solution.py:762
  114.3 42.1 %collective-permute-start = (f32[640,128]{1,0:T(8,128)S(1)}, f32[640,128]{1,0:T(8,128)S(1)}, u32[]{:S(2)}, u32[]{:S(2)}) collective-permute-start(f32[640,128]{1,0:T(8,128)S(1)} %copy-done.25), channel_id=1, source_target_pairs={{0,1},{1,0},{2,3},{3,2},{4,5},{5,4},{6,7},{7,6},{8,9},{9,8},{10,11... | collective-permute-start | bytes 983048 | tf_op jit(solution)/shard_map/ppermute | solution.py:762
  156.4 17.9 %copy-start.5 = (f32[640,128]{1,0:T(8,128)}, f32[640,128]{1,0:T(8,128)S(1)}, u32[]{:S(2)}) copy-start(f32[640,128]{1,0:T(8,128)S(1)} %collective-permute-done.near_ref) | copy-start | bytes 983044
  177.5 4.3 %collective-permute-start.9 = (f32[80,128]{1,0:T(8,128)}, f32[80,128]{1,0:T(8,128)S(1)}, u32[]{:S(2)}, u32[]{:S(2)}) collective-permute-start(f32[80,128]{1,0:T(8,128)} %get-tuple-element.38), channel_id=1, source_target_pairs={{0,1},{1,0},{2,3},{3,2},{4,5},{5,4},{6,7},{7,6},{8,9},{9,8},{10,11... | collective-permute-start | bytes 122888 | tf_op jit(solution)/shard_map/ppermute | solution.py:762
  177.6 5.6 %collective-permute-start.10 = (f32[80,128]{1,0:T(8,128)}, f32[80,128]{1,0:T(8,128)S(1)}, u32[]{:S(2)}, u32[]{:S(2)}) collective-permute-start(f32[80,128]{1,0:T(8,128)} %get-tuple-element.39), channel_id=1, source_target_pairs={{0,5},{1,4},{2,7},{3,6},{4,1},{5,0},{6,3},{7,2},{8,13},{9,12},{10,... | collective-permute-start | bytes 122888 | tf_op jit(solution)/shard_map/ppermute | solution.py:762
  178.5 17.2 %collective-permute-start.2 = (f32[240,128]{1,0:T(8,128)}, f32[240,128]{1,0:T(8,128)S(1)}, u32[]{:S(2)}, u32[]{:S(2)}) collective-permute-start(f32[240,128]{1,0:T(8,128)} %get-tuple-element.31), channel_id=1, source_target_pairs={{0,4},{1,5},{2,6},{3,7},{4,0},{5,1},{6,2},{7,3},{8,12},{9,13},{10,... | collective-permute-start | bytes 368648 | tf_op jit(solution)/shard_map/ppermute | solution.py:762
  179.7 18.0 %collective-permute-start.3 = (f32[240,128]{1,0:T(8,128)}, f32[240,128]{1,0:T(8,128)S(1)}, u32[]{:S(2)}, u32[]{:S(2)}) collective-permute-start(f32[240,128]{1,0:T(8,128)} %get-tuple-element.32), channel_id=1, source_target_pairs={{0,8},{1,9},{2,10},{3,11},{4,12},{5,13},{6,14},{7,15},{8,0},{9,1},... | collective-permute-start | bytes 368648 | tf_op jit(solution)/shard_map/ppermute | solution.py:762
  181.2 5.5 %collective-permute-start.11 = (f32[80,128]{1,0:T(8,128)}, f32[80,128]{1,0:T(8,128)S(1)}, u32[]{:S(2)}, u32[]{:S(2)}) collective-permute-start(f32[80,128]{1,0:T(8,128)} %get-tuple-element.40), channel_id=1, source_target_pairs={{0,9},{1,8},{2,11},{3,10},{4,13},{5,12},{6,15},{7,14},{8,1},{9,0},... | collective-permute-start | bytes 122888 | tf_op jit(solution)/shard_map/ppermute | solution.py:762
  181.8 24.3 %copy-start.13 = (f32[80,128]{1,0:T(8,128)}, f32[80,128]{1,0:T(8,128)S(1)}, u32[]{:S(2)}) copy-start(f32[80,128]{1,0:T(8,128)S(1)} %collective-permute-done.9.refs_8_) | copy-start | bytes 122884
  181.8 5.0 %collective-permute-start.12 = (f32[80,128]{1,0:T(8,128)}, f32[80,128]{1,0:T(8,128)S(1)}, u32[]{:S(2)}, u32[]{:S(2)}) collective-permute-start(f32[80,128]{1,0:T(8,128)} %get-tuple-element.41), channel_id=1, source_target_pairs={{0,13},{1,12},{2,15},{3,14},{4,9},{5,8},{6,11},{7,10},{8,5},{9,4},... | collective-permute-start | bytes 122888 | tf_op jit(solution)/shard_map/ppermute | solution.py:762
  183.2 22.9 %copy-start.14 = (f32[80,128]{1,0:T(8,128)}, f32[80,128]{1,0:T(8,128)S(1)}, u32[]{:S(2)}) copy-start(f32[80,128]{1,0:T(8,128)S(1)} %collective-permute-done.10.refs_9_) | copy-start | bytes 122884
  183.2 6.9 %collective-permute-start.13 = (f32[80,128]{1,0:T(8,128)}, f32[80,128]{1,0:T(8,128)S(1)}, u32[]{:S(2)}, u32[]{:S(2)}) collective-permute-start(f32[80,128]{1,0:T(8,128)} %get-tuple-element.42), channel_id=1, source_target_pairs={{0,17},{1,16},{2,19},{3,18},{4,21},{5,20},{6,23},{7,22},{8,25},{9,... | collective-permute-start | bytes 122888 | tf_op jit(solution)/shard_map/ppermute | solution.py:762
  186.7 19.4 %copy-start.15 = (f32[80,128]{1,0:T(8,128)}, f32[80,128]{1,0:T(8,128)S(1)}, u32[]{:S(2)}) copy-start(f32[80,128]{1,0:T(8,128)S(1)} %collective-permute-done.11.refs_10_) | copy-start | bytes 122884
  186.7 4.5 %collective-permute-start.14 = (f32[80,128]{1,0:T(8,128)}, f32[80,128]{1,0:T(8,128)S(1)}, u32[]{:S(2)}, u32[]{:S(2)}) collective-permute-start(f32[80,128]{1,0:T(8,128)} %get-tuple-element.43), channel_id=1, source_target_pairs={{0,21},{1,20},{2,23},{3,22},{4,17},{5,16},{6,19},{7,18},{8,29},{9,... | collective-permute-start | bytes 122888 | tf_op jit(solution)/shard_map/ppermute | solution.py:762
  186.8 19.4 %copy-start.16 = (f32[80,128]{1,0:T(8,128)}, f32[80,128]{1,0:T(8,128)S(1)}, u32[]{:S(2)}) copy-start(f32[80,128]{1,0:T(8,128)S(1)} %collective-permute-done.12.refs_11_) | copy-start | bytes 122884
  186.8 6.2 %collective-permute-start.15 = (f32[80,128]{1,0:T(8,128)}, f32[80,128]{1,0:T(8,128)S(1)}, u32[]{:S(2)}, u32[]{:S(2)}) collective-permute-start(f32[80,128]{1,0:T(8,128)} %get-tuple-element.44), channel_id=1, source_target_pairs={{0,25},{1,24},{2,27},{3,26},{4,29},{5,28},{6,31},{7,30},{8,17},{9,... | collective-permute-start | bytes 122888 | tf_op jit(solution)/shard_map/ppermute | solution.py:762
  190.0 16.1 %copy-start.17 = (f32[80,128]{1,0:T(8,128)}, f32[80,128]{1,0:T(8,128)S(1)}, u32[]{:S(2)}) copy-start(f32[80,128]{1,0:T(8,128)S(1)} %collective-permute-done.13.refs_12_) | copy-start | bytes 122884
  190.0 5.5 %collective-permute-start.16 = (f32[80,128]{1,0:T(8,128)}, f32[80,128]{1,0:T(8,128)S(1)}, u32[]{:S(2)}, u32[]{:S(2)}) collective-permute-start(f32[80,128]{1,0:T(8,128)} %get-tuple-element.45), channel_id=1, source_target_pairs={{0,29},{1,28},{2,31},{3,30},{4,25},{5,24},{6,27},{7,26},{8,21},{9,... | collective-permute-start | bytes 122888 | tf_op jit(solution)/shard_map/ppermute | solution.py:762
  191.3 14.9 %copy-start.18 = (f32[80,128]{1,0:T(8,128)}, f32[80,128]{1,0:T(8,128)S(1)}, u32[]{:S(2)}) copy-start(f32[80,128]{1,0:T(8,128)S(1)} %collective-permute-done.14.refs_13_) | copy-start | bytes 122884
  191.3 6.7 %collective-permute-start.4 = (f32[240,128]{1,0:T(8,128)}, f32[240,128]{1,0:T(8,128)S(1)}, u32[]{:S(2)}, u32[]{:S(2)}) collective-permute-start(f32[240,128]{1,0:T(8,128)} %get-tuple-element.33), channel_id=1, source_target_pairs={{0,12},{1,13},{2,14},{3,15},{4,8},{5,9},{6,10},{7,11},{8,4},{9,5},... | collective-permute-start | bytes 368648 | tf_op jit(solution)/shard_map/ppermute | solution.py:762
  192.9 13.2 %copy-start.19 = (f32[80,128]{1,0:T(8,128)}, f32[80,128]{1,0:T(8,128)S(1)}, u32[]{:S(2)}) copy-start(f32[80,128]{1,0:T(8,128)S(1)} %collective-permute-done.15.refs_14_) | copy-start | bytes 122884
  192.9 5.2 %collective-permute-start.5 = (f32[240,128]{1,0:T(8,128)}, f32[240,128]{1,0:T(8,128)S(1)}, u32[]{:S(2)}, u32[]{:S(2)}) collective-permute-start(f32[240,128]{1,0:T(8,128)} %get-tuple-element.34), channel_id=1, source_target_pairs={{0,16},{1,17},{2,18},{3,19},{4,20},{5,21},{6,22},{7,23},{8,24},{9,... | collective-permute-start | bytes 368648 | tf_op jit(solution)/shard_map/ppermute | solution.py:762
  195.5 10.6 %copy-start.20 = (f32[80,128]{1,0:T(8,128)}, f32[80,128]{1,0:T(8,128)S(1)}, u32[]{:S(2)}) copy-start(f32[80,128]{1,0:T(8,128)S(1)} %collective-permute-done.16.refs_15_) | copy-start | bytes 122884
  195.5 10.5 %collective-permute-start.6 = (f32[240,128]{1,0:T(8,128)}, f32[240,128]{1,0:T(8,128)S(1)}, u32[]{:S(2)}, u32[]{:S(2)}) collective-permute-start(f32[240,128]{1,0:T(8,128)} %get-tuple-element.35), channel_id=1, source_target_pairs={{0,20},{1,21},{2,22},{3,23},{4,16},{5,17},{6,18},{7,19},{8,28},{9,... | collective-permute-start | bytes 368648 | tf_op jit(solution)/shard_map/ppermute | solution.py:762
  195.7 10.5 %copy-start.6 = (f32[240,128]{1,0:T(8,128)}, f32[240,128]{1,0:T(8,128)S(1)}, u32[]{:S(2)}) copy-start(f32[240,128]{1,0:T(8,128)S(1)} %collective-permute-done.2.refs_1_) | copy-start | bytes 368644
  195.7 10.3 %collective-permute-start.7 = (f32[240,128]{1,0:T(8,128)}, f32[240,128]{1,0:T(8,128)S(1)}, u32[]{:S(2)}, u32[]{:S(2)}) collective-permute-start(f32[240,128]{1,0:T(8,128)} %get-tuple-element.36), channel_id=1, source_target_pairs={{0,24},{1,25},{2,26},{3,27},{4,28},{5,29},{6,30},{7,31},{8,16},{9,... | collective-permute-start | bytes 368648 | tf_op jit(solution)/shard_map/ppermute | solution.py:762
  197.7 8.4 %collective-permute-start.8 = (f32[240,128]{1,0:T(8,128)}, f32[240,128]{1,0:T(8,128)S(1)}, u32[]{:S(2)}, u32[]{:S(2)}) collective-permute-start(f32[240,128]{1,0:T(8,128)} %get-tuple-element.37), channel_id=1, source_target_pairs={{0,28},{1,29},{2,30},{3,31},{4,24},{5,25},{6,26},{7,27},{8,20},{9,... | collective-permute-start | bytes 368648 | tf_op jit(solution)/shard_map/ppermute | solution.py:762
  (14 other events, 45.4 us)

commit v3 on v2

--- a/solution.py
+++ b/solution.py
@@ -202,7 +202,8 @@
 HALF_BITS = 16
 MIDDLE = 1 << 15
 AXES = ("gx", "gy")
-WHOLE = 60 << 20
+WHOLE = 63 << 20
+PART = 24 << 20
 
 
 def real_basis(length):
@@ -252,21 +253,24 @@
                 ]
 
 
-def pack_kernel(own_ref, near_ref, far_ref, *out_refs, rows):
+def pack_kernel(own_ref, near_ref, far_ref, stats_ref, far_stats_ref, *out_refs, rows):
     pieces = len(out_refs) // 2
+    sums = stats_ref[...] + far_stats_ref[...]
     for k in range(pieces):
         block = slice(k * rows, (k + 1) * rows)
         out_refs[k][0:rows, :] = own_ref[block, :]
         out_refs[k][rows : 2 * rows, :] = near_ref[block, :]
         out_refs[k][2 * rows : 3 * rows, :] = far_ref[block, :]
-        out_refs[pieces + k][...] = far_ref[(pieces + k) * rows : (pieces + k + 1) * rows, :]
-
-
-def z_inverse_kernel(*refs, q_count, block, groups, devices, rows, last_rows, direct, gy_size, cell_total):
+        out_refs[k][3 * rows :, :] = sums
+        out_refs[pieces + k][:rows, :] = far_ref[(pieces + k) * rows : (pieces + k + 1) * rows, :]
+        out_refs[pieces + k][rows:, :] = sums
+
+
+def z_inverse_kernel(*refs, q_count, block, groups, devices, rows, direct, gy_size, cell_total):
     gx_size = devices // gy_size
     pieces, refs = refs[: 2 * gx_size], refs[2 * gx_size :]
     direct_refs, refs = refs[:direct], refs[direct:]
-    basis_ref, out_ref, stress_ref, energy_ref, first_ref = refs
+    basis_ref, out_ref, stress_ref, energy_ref, first_ref, sums_ref = refs
     basis = basis_ref[...]
 
     @pl.when(pl.program_id(0) == 0)
@@ -278,17 +282,15 @@
                 first_ref[pl.ds(pl.multiple_of(source * rows, SUBLANES), rows), :] = piece[
                     b * rows : (b + 1) * rows, :
                 ]
-        last = direct_refs[-1]
-        total = None
-        for d in range(devices):
-            part = last[(d + 1) * last_rows - SUBLANES : (d + 1) * last_rows, :]
-            total = part if total is None else total + part
+            pair = (my_x ^ (k % gx_size)) * 2 + (my_y ^ (k // gx_size)) % 2
+            sums_ref[pl.ds(pl.multiple_of(pair * SUBLANES, SUBLANES), SUBLANES), :] = piece[-SUBLANES:, :]
+        total = jnp.sum(sums_ref[...].reshape(devices // 2, SUBLANES, LANES), axis=0)
         terms = [jnp.sum(total[k : k + 1, :]) for k in range(STATS)]
         energy_ref[0, 0] = terms[0] * (0.5 / cell_total)
         for k, term in enumerate((0, 3, 4, 3, 1, 5, 4, 5, 2)):
             stress_ref[k // 3, k % 3] = terms[term + 1] * (-0.5 / cell_total)
 
-    sources = [(first_ref, rows)] + [(ref, last_rows if ref is direct_refs[-1] else rows) for ref in direct_refs]
+    sources = [(ref, rows) for ref in (first_ref, *direct_refs)]
     for k in range(block):
         q = pl.program_id(0) * block + k
         for g in range(groups):
@@ -391,7 +393,6 @@
     gx_size,
     gy_size,
     rows,
-    out_rows,
     half,
     n_tables,
     hopped,
@@ -403,14 +404,27 @@
     special = slot == 0
     out_refs, rest = rest[: 1 + 2 * hopped], rest[1 + 2 * hopped :]
     stats_ref, y_wide_ref, y_back_wide_ref, rows_ref, spectrum_ref, u_ref, tables_ref, sem = rest
-    first_copy = pltpu.make_async_copy(tables[0], tables_ref.at[0], sem.at[0])
-    first_copy.start()
-    if n_tables > 1:
-        second_copy = pltpu.make_async_copy(tables[1], tables_ref.at[1], sem.at[1])
-
-        @pl.when(special)
-        def _():
-            second_copy.start()
+    blocks = half // SUBLANES + 1
+    table_order = [blocks - 1, *range(blocks - 1)]
+
+    def table_copy(k, block):
+        return pltpu.make_async_copy(tables[k].at[block], tables_ref.at[k, block], sem.at[k, block])
+
+    for block in table_order:
+        table_copy(0, block).start()
+        if n_tables > 1:
+
+            @pl.when(special)
+            def _(block=block):
+                table_copy(1, block).start()
+
+    def wait_table(block):
+        table_copy(0, block).wait()
+        if n_tables > 1:
+
+            @pl.when(special)
+            def _():
+                table_copy(1, block).wait()
 
     full = 2 * half
     local_y = full // gy_size
@@ -464,13 +478,7 @@
         for i in range(2):
             spectrum_ref[(first + i) * full : (first + i + 1) * full, :] = result[:, i * full : (i + 1) * full]
 
-    first_copy.wait()
-    if n_tables > 1:
-
-        @pl.when(special)
-        def _():
-            second_copy.wait()
-
+    wait_table(blocks - 1)
     wave = math.pi / half
     lane = lax.broadcasted_iota(jnp.int32, (SUBLANES, LANES), 1)
     row = lax.broadcasted_iota(jnp.int32, (SUBLANES, LANES), 0)
@@ -492,6 +500,7 @@
 
     def one_block(block, carry):
         energy, xx, yy, zz, xy, xz, yz = carry
+        wait_table(block)
         top = pl.multiple_of(block * SUBLANES, SUBLANES)
         tops = (block, jnp.where(block == 0, half // SUBLANES, block))
         values = {}
@@ -582,10 +591,8 @@
                     out_refs[2][pl.ds(top, rows), :] = value
 
             else:
-                top = (x * gy_size + s) * out_rows
+                top = (x * gy_size + s) * rows
                 out_refs[0][top : top + rows, :] = value
-                if out_rows > rows:
-                    out_refs[0][top + rows : top + out_rows, :] = stats_ref[...]
 
 
 def table_rows(phi_table, dphi_table, q_count, padded):
@@ -719,13 +726,15 @@
         for part in (high, low)
     ]
     y_back = jnp.asarray(np.stack([wide[0], wide[0], wide[1]]))
+
+    def hop(value, step):
+        return lax.ppermute(value, AXES, [(d, d ^ step) for d in range(devices)])
+
     returned = []
-    last_rows = rows + SUBLANES
     stats = ()
     for c in range(slots):
         hopped = c == 0
-        out_rows = last_rows if c == slots - 1 else rows
-        outs = [devices * out_rows]
+        outs = [devices * rows]
         if hopped:
             outs = [gx_size * rows, gx_size * rows, 2 * gx_size * rows]
         *back, part = pl.pallas_call(
@@ -735,7 +744,6 @@
                 gx_size=gx_size,
                 gy_size=gy_size,
                 rows=rows,
-                out_rows=out_rows,
                 half=half,
                 base=(slots - 1 - c) * devices,
                 n_tables=len(tables[c]),
@@ -752,29 +760,15 @@
                 pltpu.VMEM((2 * q_count * full, LANES), jnp.float32),
                 pltpu.VMEM((2 * q_count * full, LANES), jnp.float32),
                 pltpu.VMEM((len(tables[c]), blocks, pairs, SUBLANES, LANES), jnp.float32),
-                pltpu.SemaphoreType.DMA((len(tables[c]),)),
+                pltpu.SemaphoreType.DMA((len(tables[c]), blocks)),
             ],
             compiler_params=pltpu.CompilerParams(vmem_limit_bytes=WHOLE),
             name="planes",
         )(arrived[c], y_forward, y_back, x_forward, x_back, *stats, *tables[c])
         if hopped:
-            def hop(value, step):
-                return lax.ppermute(value, AXES, [(d, d ^ step) for d in range(devices)])
-
+            own = back[0]
             far = hop(back[2], 2)
             near = hop(back[1], 1)
-            gathered = pl.pallas_call(
-                functools.partial(pack_kernel, rows=rows),
-                in_specs=[vmem] * 3,
-                out_specs=(vmem,) * (2 * gx_size),
-                out_shape=(jax.ShapeDtypeStruct((3 * rows, LANES), jnp.float32),) * gx_size
-                + (jax.ShapeDtypeStruct((rows, LANES), jnp.float32),) * gx_size,
-                compiler_params=pltpu.CompilerParams(vmem_limit_bytes=WHOLE),
-                name="pack",
-            )(back[0], near, far)
-            gathered = list(gathered)
-            for k in [*range(gx_size, 2 * gx_size), *range(1, gx_size)]:
-                gathered[k] = hop(gathered[k], k % gx_size * gy_size + k // gx_size)
             stats = (
                 pl.pallas_call(
                     mark_kernel,
@@ -785,7 +779,21 @@
                 )(part),
             )
         else:
+            far_part = hop(part, 2)
             returned.append(swap(back[0], devices))
+
+    gathered = pl.pallas_call(
+        functools.partial(pack_kernel, rows=rows),
+        in_specs=[vmem] * 5,
+        out_specs=(vmem,) * (2 * gx_size),
+        out_shape=(jax.ShapeDtypeStruct((3 * rows + SUBLANES, LANES), jnp.float32),) * gx_size
+        + (jax.ShapeDtypeStruct((rows + SUBLANES, LANES), jnp.float32),) * gx_size,
+        compiler_params=pltpu.CompilerParams(vmem_limit_bytes=PART),
+        name="pack",
+    )(own, near, far, part, far_part)
+    gathered = list(gathered)
+    for k in [*range(gx_size, 2 * gx_size), *range(1, gx_size)]:
+        gathered[k] = hop(gathered[k], k % gx_size * gy_size + k // gx_size)
 
     high, low = halves(np.concatenate([z_basis[rows_of] for rows_of in order], axis=0))
     block = max(k for k in range(1, 6) if q_count % k == 0)
@@ -797,7 +805,6 @@
             groups=groups,
             devices=devices,
             rows=rows,
-            last_rows=last_rows,
             direct=len(returned),
             gy_size=gy_size,
             cell_total=cell_total,
@@ -815,8 +822,11 @@
             jax.ShapeDtypeStruct((3, 3), jnp.float32),
             jax.ShapeDtypeStruct((1, 1), jnp.float32),
         ),
-        scratch_shapes=[pltpu.VMEM((devices * rows, LANES), jnp.float32)],
-        compiler_params=pltpu.CompilerParams(vmem_limit_bytes=WHOLE),
+        scratch_shapes=[
+            pltpu.VMEM((devices * rows, LANES), jnp.float32),
+            pltpu.VMEM((devices // 2 * SUBLANES, LANES), jnp.float32),
+        ],
+        compiler_params=pltpu.CompilerParams(vmem_limit_bytes=PART),
         name="z_inverse",
     )(*gathered, *returned, jnp.asarray(np.concatenate([high, high, low], axis=0)))
     return (u_grids.reshape(theta.shape), stress, energy.reshape(()))

time: 213 us -> 202 us (0.948)
  Pallas kernels: 73.2 us -> 66.6 us
  waiting for transfers between devices: 99 us -> 95.8 us
    ppermute x17 -> x18, waiting for transfers between devices: 72.6 us -> 69.4 us  [hop(): return lax.ppermute(value, AXES, [(d, d ^ step) for d in range(devices)])]
    pallas_call x2, Pallas kernels: 20.6 us -> 18 us  [real_shards(): pl.pallas_call(functools.partial(plane_kernel, q_count=q_count, gx_size=g...]
    pallas_call x1, Pallas kernels: 2.39 us -> 0.1 us  [real_shards(): pl.pallas_call(functools.partial(pack_kernel, rows=rows), in_specs=[vmem]...]
    ppermute x17 -> x18, starting transfers between devices: 18.4 us -> 19.2 us  [hop(): return lax.ppermute(value, AXES, [(d, d ^ step) for d in range(devices)])]
  transfers between devices with their start and end apart: 20 -> 21, of which waited for: 10 -> 9; matrix products, arithmetic and copies ran while one was open for 1% -> 1% of each run, Pallas kernels for 25% -> 25%
where the time goes in v3:
time: 202 us; the launch traced here: 201 us
  waiting for transfers between devices  95.8 us (47%)
  Pallas kernels  66.6 us (33%)
  starting transfers between devices  34.3 us (17%)
  local copies, waits for them, and re-layouts  2.96 us (1%)
    ppermute x18, waiting for transfers between devices, hop(): return lax.ppermute(value, AXES, [(d, d ^ step) for d in range(devices)])  69.4 us
    all_to_all x3, waiting for transfers between devices, swap(): lax.all_to_all(parts, AXES, split_axis=0, concat_axis=0, tiled=True)  26.4 us
    pallas_call x2, Pallas kernels, real_shards(): pl.pallas_call(functools.partial(table_kernel, **sizes), in_specs=[smem,...  25.9 us
    ppermute x18, starting transfers between devices, hop(): return lax.ppermute(value, AXES, [(d, d ^ step) for d in range(devices)])  19.2 us
    pallas_call x2, Pallas kernels, real_shards(): pl.pallas_call(functools.partial(plane_kernel, q_count=q_count, gx_size=g...  18 us
    all_to_all x3, starting transfers between devices, swap(): lax.all_to_all(parts, AXES, split_axis=0, concat_axis=0, tiled=True)  15.2 us
    pallas_call x1, Pallas kernels, real_shards(): pl.pallas_call(functools.partial(second_table_kernel, **sizes), in_specs=...  10.4 us
    pallas_call x2, Pallas kernels, real_shards(): pl.pallas_call(functools.partial(z_forward_kernel, q_count=q_count, block...  7.95 us
  transfers between devices with their start and end apart: 21, of which 9 were waited for; matrix products, arithmetic and copies ran while one was open for 1% of the time, Pallas kernels for 25%

profile of v3, /device:TPU:0, one launch (start us, length us, event | category | flops | bytes accessed | tf_op | source)
XLA Modules:
  0.0 201.0 jit_solution(3189095217786476237)
XLA Ops:
  0.6 4.0 %z_forward.2 = f32[2560,128]{1,0:T(8,128)} custom-call(f32[10,512,128]{2,1,0:T(8,128)} %bitcast.21, bf16[64,384]{1,0:T(8,128)(2,1)} %constant.41.clone.basis_ref), custom_call_target="tpu_custom_call" | custom-call | tf_op jit(solution)/shard_map/z_forward/pallas_call | solution.py:654
  4.6 7.4 %all-to-all-start = ((f32[32,80,128]{2,1,0:T(8,128)}), f32[32,80,128]{2,1,0:T(8,128)}, u32[]{:S(2)}, u32[]{:S(2)}) async-start(f32[32,80,128]{2,1,0:T(8,128)} %bitcast.24), calls=%async_computation | async-start | bytes 2621440 | tf_op jit(solution)/shard_map/all_to_all | solution.py:616
  12.1 4.0 %z_forward.3 = f32[2560,128]{1,0:T(8,128)} custom-call(f32[10,512,128]{2,1,0:T(8,128)} %bitcast.22, bf16[64,384]{1,0:T(8,128)(2,1)} %constant.42.clone.basis_ref), custom_call_target="tpu_custom_call" | custom-call | tf_op jit(solution)/shard_map/z_forward/pallas_call | solution.py:654
  16.0 26.4 %all-to-all-done = f32[32,80,128]{2,1,0:T(8,128)} async-done(((f32[32,80,128]{2,1,0:T(8,128)}), f32[32,80,128]{2,1,0:T(8,128)}, u32[]{:S(2)}, u32[]{:S(2)}) %all-to-all-start) | async-done | bytes 1310752 | tf_op jit(solution)/shard_map/all_to_all | solution.py:616
  42.5 4.8 %all-to-all-start.1 = ((f32[32,80,128]{2,1,0:T(8,128)}), f32[32,80,128]{2,1,0:T(8,128)}, u32[]{:S(2)}, u32[]{:S(2)}) async-start(f32[32,80,128]{2,1,0:T(8,128)} %bitcast.23), calls=%async_computation.1 | async-start | bytes 2621440 | tf_op jit(solution)/shard_map/all_to_all | solution.py:616
  47.3 0.7 gather_fusion
  48.0 0.7 gather_fusion.1
  49.8 0.9 bitcast_bitcast_fusion.words_ref
  50.7 12.1 %kernel_table.2.rest_0_ = f32[9,155,8,128]{3,2,1,0:T(8,128)} custom-call(s32[1170]{0:T(1024)} %constant.46.clone.bounds_ref, f32[155]{0:T(256)} %copy-done.5, s32[8,160,128]{2,1,0:T(8,128)} %bitcast_bitcast_fusion.words_ref), custom_call_target="tpu_custom_call" | custom-call | tf_op jit(solution)/shard_map/kernel_table/pallas_call | solution.py:690
  62.8 13.8 %kernel_table.3.rest_1_ = f32[9,155,8,128]{3,2,1,0:T(8,128)} custom-call(s32[1170]{0:T(1024)} %constant.46.clone.bounds_ref, f32[155]{0:T(256)} %copy-done.5, s32[8,160,128]{2,1,0:T(8,128)} %bitcast_bitcast_fusion.words_ref), custom_call_target="tpu_custom_call" | custom-call | tf_op jit(solution)/shard_map/kernel_table/pallas_call | solution.py:690
  76.6 10.4 %second_table.1.rest_2_ = f32[9,155,8,128]{3,2,1,0:T(8,128)} custom-call(s32[1170]{0:T(1024)} %constant.46.clone.bounds_ref, f32[155]{0:T(256)} %copy-done.5, s32[8,160,128]{2,1,0:T(8,128)} %bitcast_bitcast_fusion.words_ref), custom_call_target="tpu_custom_call" | custom-call | tf_op jit(solution)/shard_map/second_table/pallas_call | solution.py:702
  87.1 9.0 %planes.2 = (f32[640,128]{1,0:T(8,128)}, f32[640,128]{1,0:T(8,128)}, f32[1280,128]{1,0:T(8,128)}, f32[8,128]{1,0:T(8,128)}) custom-call(f32[2560,128]{1,0:T(8,128)} %bitcast.2.sent_ref, bf16[3,128,128]{2,1,0:T(8,128)(2,1)} %constant.49.clone.y_ref, bf16[3,128,512]{2,1,0:T(8,128)(2,1)} %constant.50.clone.y_back_ref, bf16[128,384]{1,0:T(8,128)(2,1)} %constant.47.clone.x_ref, ...), custom_call_target="tpu_custom_call" | custom-call | tf_op jit(solution)/shard_map/planes/pallas_call | solution.py:740
  96.1 1.3 mark.1.rest_0_
  97.4 8.9 %planes.3 = (f32[2560,128]{1,0:T(8,128)}, f32[8,128]{1,0:T(8,128)}) custom-call(f32[2560,128]{1,0:T(8,128)} %bitcast.7.sent_ref, bf16[3,128,128]{2,1,0:T(8,128)(2,1)} %constant.49.clone.y_ref, bf16[3,128,512]{2,1,0:T(8,128)(2,1)} %constant.50.clone.y_back_ref, bf16[128,384]{1,0:T(8,128)(2,1)} %constant.47.clone.x_ref, ...), custom_call_target="tpu_custom_call" | custom-call | tf_op jit(solution)/shard_map/planes/pallas_call | solution.py:740
  106.3 3.0 %all-to-all-start.2 = ((f32[32,80,128]{2,1,0:T(8,128)}), f32[32,80,128]{2,1,0:T(8,128)S(1)}, u32[]{:S(2)}, u32[]{:S(2)}) async-start(f32[32,80,128]{2,1,0:T(8,128)} %bitcast.27), calls=%async_computation.2 | async-start | bytes 2621440 | tf_op jit(solution)/shard_map/all_to_all | solution.py:616
  109.4 2.5 %collective-permute-start.1 = (f32[1280,128]{1,0:T(8,128)}, f32[1280,128]{1,0:T(8,128)S(1)}, u32[]{:S(2)}, u32[]{:S(2)}) collective-permute-start(f32[1280,128]{1,0:T(8,128)} %get-tuple-element.30), channel_id=1, source_target_pairs={{0,2},{1,3},{2,0},{3,1},{4,6},{5,7},{6,4},{7,5},{8,10},{9,11},{10,... | collective-permute-start | bytes 1966088 | tf_op jit(solution)/shard_map/ppermute | solution.py:731
  111.9 1.5 collective-permute-start
  113.9 55.4 %collective-permute-done.2.far_stats_ref = f32[8,128]{1,0:T(8,128)S(1)} collective-permute-done((f32[8,128]{1,0:T(8,128)S(1)}, f32[8,128]{1,0:T(8,128)S(1)}, u32[]{:S(2)}, u32[]{:S(2)}) %collective-permute-start.2) | collective-permute-done | bytes 4128 | tf_op jit(solution)/shard_map/ppermute | solution.py:731
  169.4 0.9 collective-permute-start.11
  170.3 1.2 collective-permute-start.3
  171.6 1.5 collective-permute-start.4
  173.5 1.6 collective-permute-start.13
  175.0 1.3 collective-permute-start.14
  176.4 2.0 collective-permute-done.12.refs_10_
  178.4 3.4 %collective-permute-start.16 = (f32[88,128]{1,0:T(8,128)S(1)}, f32[88,128]{1,0:T(8,128)S(1)}, u32[]{:S(2)}, u32[]{:S(2)}) collective-permute-start(f32[88,128]{1,0:T(8,128)S(1)} %get-tuple-element.47), channel_id=1, source_target_pairs={{0,25},{1,24},{2,27},{3,26},{4,29},{5,28},{6,31},{7,30},{8,17},{9,... | collective-permute-start | bytes 135176 | tf_op jit(solution)/shard_map/ppermute | solution.py:731
  183.2 1.3 collective-permute-done.16.refs_14_
  184.5 1.2 collective-permute-start.6
  185.7 1.4 collective-permute-done.17.refs_15_
  187.3 1.8 collective-permute-start.8
  189.0 0.6 collective-permute-start.9
  189.9 8.2 %collective-permute-done.7.refs_5_ = f32[248,128]{1,0:T(8,128)S(1)} collective-permute-done((f32[248,128]{1,0:T(8,128)S(1)}, f32[248,128]{1,0:T(8,128)S(1)}, u32[]{:S(2)}, u32[]{:S(2)}) %collective-permute-start.7) | collective-permute-done | bytes 127008 | tf_op jit(solution)/shard_map/ppermute | solution.py:731
  198.0 3.0 %z_inverse.1 = (f32[10,512,128]{2,1,0:T(8,128)}, f32[3,3]{1,0:T(4,128)}, f32[1,1]{1,0:T(1,128)}) custom-call(f32[248,128]{1,0:T(8,128)S(1)} %get-tuple-element.33.refs_0_, f32[248,128]{1,0:T(8,128)S(1)} %collective-permute-done.3.refs_1_, f32[248,128]{1,0:T(8,128)S(1)} %collective-permute-done.4.refs_2_, f32[248,128]{1,0:T(8,128)S(1)} %collective-permute-done.5.refs_3_, ...), custom_call_target="tpu_custom_call" | custom-call | tf_op jit(solution)/shard_map/z_inverse/pallas_call | solution.py:800
  (50 shorter events, 4.1 us)
Async XLA Ops:
  0.6 46.6 %copy-start = (f32[1024,100]{0,1:T(8,128)S(1)}, f32[1024,100]{0,1:T(8,128)}, u32[]{:S(2)}) copy-start(f32[1024,100]{0,1:T(8,128)} %param.17) | copy-start | bytes 1228804
  4.6 37.8 %all-to-all-start = ((f32[32,80,128]{2,1,0:T(8,128)}), f32[32,80,128]{2,1,0:T(8,128)}, u32[]{:S(2)}, u32[]{:S(2)}) async-start(f32[32,80,128]{2,1,0:T(8,128)} %bitcast.24), calls=%async_computation | async-start | bytes 2621440 | tf_op jit(solution)/shard_map/all_to_all | solution.py:616
  42.4 4.8 %copy-start.7 = (s32[55]{0:T(128)S(1)}, s32[55]{0:T(128)}, u32[]{:S(2)}) copy-start(s32[55]{0:T(128)} %constant.56) | copy-start | bytes 664
  42.5 54.9 %all-to-all-start.1 = ((f32[32,80,128]{2,1,0:T(8,128)}), f32[32,80,128]{2,1,0:T(8,128)}, u32[]{:S(2)}, u32[]{:S(2)}) async-start(f32[32,80,128]{2,1,0:T(8,128)} %bitcast.23), calls=%async_computation.1 | async-start | bytes 2621440 | tf_op jit(solution)/shard_map/all_to_all | solution.py:616
  47.2 0.7 copy-start.6
  47.9 1.0 copy-start.4
  49.1 0.6 copy-start.5
  106.3 5.6 %copy-start.8 = (f32[640,128]{1,0:T(8,128)S(1)}, f32[640,128]{1,0:T(8,128)}, u32[]{:S(2)}) copy-start(f32[640,128]{1,0:T(8,128)} %get-tuple-element.29) | copy-start | bytes 983044
  106.3 7.1 %copy-start.3 = (f32[8,128]{1,0:T(8,128)S(1)}, f32[8,128]{1,0:T(8,128)}, u32[]{:S(2)}) copy-start(f32[8,128]{1,0:T(8,128)} %get-tuple-element.32.stats_ref) | copy-start | bytes 12292
  106.3 62.9 %copy-start.1 = (f32[640,128]{1,0:T(8,128)S(1)}, f32[640,128]{1,0:T(8,128)}, u32[]{:S(2)}) copy-start(f32[640,128]{1,0:T(8,128)} %get-tuple-element.28.own_ref) | copy-start | bytes 983044
  106.3 91.7 %all-to-all-start.2 = ((f32[32,80,128]{2,1,0:T(8,128)}), f32[32,80,128]{2,1,0:T(8,128)S(1)}, u32[]{:S(2)}, u32[]{:S(2)}) async-start(f32[32,80,128]{2,1,0:T(8,128)} %bitcast.27), calls=%async_computation.2 | async-start | bytes 2621440 | tf_op jit(solution)/shard_map/all_to_all | solution.py:616
  109.4 88.7 %copy-start.2 = (bf16[384,128]{1,0:T(8,128)(2,1)S(1)}, bf16[384,128]{1,0:T(8,128)(2,1)}, u32[]{:S(2)}) copy-start(bf16[384,128]{1,0:T(8,128)(2,1)} %constant.51.clone.refs_17_) | copy-start | bytes 294916
  109.4 59.9 %collective-permute-start.1 = (f32[1280,128]{1,0:T(8,128)}, f32[1280,128]{1,0:T(8,128)S(1)}, u32[]{:S(2)}, u32[]{:S(2)}) collective-permute-start(f32[1280,128]{1,0:T(8,128)} %get-tuple-element.30), channel_id=1, source_target_pairs={{0,2},{1,3},{2,0},{3,1},{4,6},{5,7},{6,4},{7,5},{8,10},{9,11},{10,... | collective-permute-start | bytes 1966088 | tf_op jit(solution)/shard_map/ppermute | solution.py:731
  111.9 57.3 %collective-permute-start = (f32[640,128]{1,0:T(8,128)S(1)}, f32[640,128]{1,0:T(8,128)S(1)}, u32[]{:S(2)}, u32[]{:S(2)}) collective-permute-start(f32[640,128]{1,0:T(8,128)S(1)} %copy-done.8), channel_id=1, source_target_pairs={{0,1},{1,0},{2,3},{3,2},{4,5},{5,4},{6,7},{7,6},{8,9},{9,8},{10,11... | collective-permute-start | bytes 983048 | tf_op jit(solution)/shard_map/ppermute | solution.py:731
  113.4 55.8 %collective-permute-start.2 = (f32[8,128]{1,0:T(8,128)S(1)}, f32[8,128]{1,0:T(8,128)S(1)}, u32[]{:S(2)}, u32[]{:S(2)}) collective-permute-start(f32[8,128]{1,0:T(8,128)S(1)} %copy-done.3), channel_id=1, source_target_pairs={{0,2},{1,3},{2,0},{3,1},{4,6},{5,7},{6,4},{7,5},{8,10},{9,11},{10,... | collective-permute-start | bytes 12296 | tf_op jit(solution)/shard_map/ppermute | solution.py:731
  169.4 4.1 %collective-permute-start.10 = (f32[88,128]{1,0:T(8,128)S(1)}, f32[88,128]{1,0:T(8,128)S(1)}, u32[]{:S(2)}, u32[]{:S(2)}) collective-permute-start(f32[88,128]{1,0:T(8,128)S(1)} %get-tuple-element.41), channel_id=1, source_target_pairs={{0,1},{1,0},{2,3},{3,2},{4,5},{5,4},{6,7},{7,6},{8,9},{9,8},{10,11... | collective-permute-start | bytes 135176 | tf_op jit(solution)/shard_map/ppermute | solution.py:731
  169.4 5.6 %collective-permute-start.11 = (f32[88,128]{1,0:T(8,128)S(1)}, f32[88,128]{1,0:T(8,128)S(1)}, u32[]{:S(2)}, u32[]{:S(2)}) collective-permute-start(f32[88,128]{1,0:T(8,128)S(1)} %get-tuple-element.42), channel_id=1, source_target_pairs={{0,5},{1,4},{2,7},{3,6},{4,1},{5,0},{6,3},{7,2},{8,13},{9,12},{10,... | collective-permute-start | bytes 135176 | tf_op jit(solution)/shard_map/ppermute | solution.py:731
  170.3 16.9 %collective-permute-start.3 = (f32[248,128]{1,0:T(8,128)S(1)}, f32[248,128]{1,0:T(8,128)S(1)}, u32[]{:S(2)}, u32[]{:S(2)}) collective-permute-start(f32[248,128]{1,0:T(8,128)S(1)} %get-tuple-element.34), channel_id=1, source_target_pairs={{0,4},{1,5},{2,6},{3,7},{4,0},{5,1},{6,2},{7,3},{8,12},{9,13},{10,... | collective-permute-start | bytes 380936 | tf_op jit(solution)/shard_map/ppermute | solution.py:731
  171.6 17.4 %collective-permute-start.4 = (f32[248,128]{1,0:T(8,128)S(1)}, f32[248,128]{1,0:T(8,128)S(1)}, u32[]{:S(2)}, u32[]{:S(2)}) collective-permute-start(f32[248,128]{1,0:T(8,128)S(1)} %get-tuple-element.35), channel_id=1, source_target_pairs={{0,8},{1,9},{2,10},{3,11},{4,12},{5,13},{6,14},{7,15},{8,0},{9,1},... | collective-permute-start | bytes 380936 | tf_op jit(solution)/shard_map/ppermute | solution.py:731
  173.1 5.3 %collective-permute-start.12 = (f32[88,128]{1,0:T(8,128)S(1)}, f32[88,128]{1,0:T(8,128)S(1)}, u32[]{:S(2)}, u32[]{:S(2)}) collective-permute-start(f32[88,128]{1,0:T(8,128)S(1)} %get-tuple-element.43), channel_id=1, source_target_pairs={{0,9},{1,8},{2,11},{3,10},{4,13},{5,12},{6,15},{7,14},{8,1},{9,0},... | collective-permute-start | bytes 135176 | tf_op jit(solution)/shard_map/ppermute | solution.py:731
  173.5 4.9 %collective-permute-start.13 = (f32[88,128]{1,0:T(8,128)S(1)}, f32[88,128]{1,0:T(8,128)S(1)}, u32[]{:S(2)}, u32[]{:S(2)}) collective-permute-start(f32[88,128]{1,0:T(8,128)S(1)} %get-tuple-element.44), channel_id=1, source_target_pairs={{0,13},{1,12},{2,15},{3,14},{4,9},{5,8},{6,11},{7,10},{8,5},{9,4},... | collective-permute-start | bytes 135176 | tf_op jit(solution)/shard_map/ppermute | solution.py:731
  175.0 6.7 %collective-permute-start.14 = (f32[88,128]{1,0:T(8,128)S(1)}, f32[88,128]{1,0:T(8,128)S(1)}, u32[]{:S(2)}, u32[]{:S(2)}) collective-permute-start(f32[88,128]{1,0:T(8,128)S(1)} %get-tuple-element.45), channel_id=1, source_target_pairs={{0,17},{1,16},{2,19},{3,18},{4,21},{5,20},{6,23},{7,22},{8,25},{9,... | collective-permute-start | bytes 135176 | tf_op jit(solution)/shard_map/ppermute | solution.py:731
  178.3 4.4 %collective-permute-start.15 = (f32[88,128]{1,0:T(8,128)S(1)}, f32[88,128]{1,0:T(8,128)S(1)}, u32[]{:S(2)}, u32[]{:S(2)}) collective-permute-start(f32[88,128]{1,0:T(8,128)S(1)} %get-tuple-element.46), channel_id=1, source_target_pairs={{0,21},{1,20},{2,23},{3,22},{4,17},{5,16},{6,19},{7,18},{8,29},{9,... | collective-permute-start | bytes 135176 | tf_op jit(solution)/shard_map/ppermute | solution.py:731
  178.4 6.1 %collective-permute-start.16 = (f32[88,128]{1,0:T(8,128)S(1)}, f32[88,128]{1,0:T(8,128)S(1)}, u32[]{:S(2)}, u32[]{:S(2)}) collective-permute-start(f32[88,128]{1,0:T(8,128)S(1)} %get-tuple-element.47), channel_id=1, source_target_pairs={{0,25},{1,24},{2,27},{3,26},{4,29},{5,28},{6,31},{7,30},{8,17},{9,... | collective-permute-start | bytes 135176 | tf_op jit(solution)/shard_map/ppermute | solution.py:731
  181.8 5.4 %collective-permute-start.17 = (f32[88,128]{1,0:T(8,128)S(1)}, f32[88,128]{1,0:T(8,128)S(1)}, u32[]{:S(2)}, u32[]{:S(2)}) collective-permute-start(f32[88,128]{1,0:T(8,128)S(1)} %get-tuple-element.48), channel_id=1, source_target_pairs={{0,29},{1,28},{2,31},{3,30},{4,25},{5,24},{6,27},{7,26},{8,21},{9,... | collective-permute-start | bytes 135176 | tf_op jit(solution)/shard_map/ppermute | solution.py:731
  182.7 6.9 %collective-permute-start.5 = (f32[248,128]{1,0:T(8,128)S(1)}, f32[248,128]{1,0:T(8,128)S(1)}, u32[]{:S(2)}, u32[]{:S(2)}) collective-permute-start(f32[248,128]{1,0:T(8,128)S(1)} %get-tuple-element.36), channel_id=1, source_target_pairs={{0,12},{1,13},{2,14},{3,15},{4,8},{5,9},{6,10},{7,11},{8,4},{9,5},... | collective-permute-start | bytes 380936 | tf_op jit(solution)/shard_map/ppermute | solution.py:731
  184.5 5.4 %collective-permute-start.6 = (f32[248,128]{1,0:T(8,128)S(1)}, f32[248,128]{1,0:T(8,128)S(1)}, u32[]{:S(2)}, u32[]{:S(2)}) collective-permute-start(f32[248,128]{1,0:T(8,128)S(1)} %get-tuple-element.37), channel_id=1, source_target_pairs={{0,16},{1,17},{2,18},{3,19},{4,20},{5,21},{6,22},{7,23},{8,24},{9,... | collective-permute-start | bytes 380936 | tf_op jit(solution)/shard_map/ppermute | solution.py:731
  187.2 10.9 %collective-permute-start.7 = (f32[248,128]{1,0:T(8,128)S(1)}, f32[248,128]{1,0:T(8,128)S(1)}, u32[]{:S(2)}, u32[]{:S(2)}) collective-permute-start(f32[248,128]{1,0:T(8,128)S(1)} %get-tuple-element.38), channel_id=1, source_target_pairs={{0,20},{1,21},{2,22},{3,23},{4,16},{5,17},{6,18},{7,19},{8,28},{9,... | collective-permute-start | bytes 380936 | tf_op jit(solution)/shard_map/ppermute | solution.py:731
  187.3 10.8 %collective-permute-start.8 = (f32[248,128]{1,0:T(8,128)S(1)}, f32[248,128]{1,0:T(8,128)S(1)}, u32[]{:S(2)}, u32[]{:S(2)}) collective-permute-start(f32[248,128]{1,0:T(8,128)S(1)} %get-tuple-element.39), channel_id=1, source_target_pairs={{0,24},{1,25},{2,26},{3,27},{4,28},{5,29},{6,30},{7,31},{8,16},{9,... | collective-permute-start | bytes 380936 | tf_op jit(solution)/shard_map/ppermute | solution.py:731
  189.0 9.0 %collective-permute-start.9 = (f32[248,128]{1,0:T(8,128)S(1)}, f32[248,128]{1,0:T(8,128)S(1)}, u32[]{:S(2)}, u32[]{:S(2)}) collective-permute-start(f32[248,128]{1,0:T(8,128)S(1)} %get-tuple-element.40), channel_id=1, source_target_pairs={{0,28},{1,29},{2,30},{3,31},{4,24},{5,25},{6,26},{7,27},{8,20},{9,... | collective-permute-start | bytes 380936 | tf_op jit(solution)/shard_map/ppermute | solution.py:731
